TPU v7x, 32 devices: a whole 2x2x4 slice. The times are simulated.
32 devices in a mesh: gx: 8 (over y, x, core), gy: 4 (over z).
Axes of the slice: x: 2, y: 2, z: 4, core: 2. Of those that a mesh axis runs over, the one named last changes fastest.
Arguments:
- core_one: bfloat16 [200, 128], replicated, may hold values from -6 to 6
- core_two: bfloat16 [200, 4096], replicated, may hold values from -1 to 1
- core_three: bfloat16 [250, 256], replicated, may hold values from -1 to 1
- dense_rows: bfloat16 [2048, 128], P(('gx', 'gy')), may hold values from -6 to 6
- w_top: bfloat16 [256, 256], replicated, may hold values from -0.375 to 0.375
- bias_top: float32 [256], replicated, may hold values from -3 to 3
- w_out: float32 [256], replicated, may hold values from -0.75 to 0.75
- labels: int32 [2048], P(('gx', 'gy')), may hold values 0 or 1
- bag_ids: int32 [32, 256], P(('gx', 'gy')), may hold values from 0 to 63, never falling along the last dimension, each value on 1 to 8 neighbouring positions
- digit_one: int32 [32, 256], P(('gx', 'gy')), may hold values from 0 to 199
- digit_two: int32 [32, 256], P(('gx', 'gy')), may hold values from 0 to 199
- digit_three: int32 [32, 256], P(('gx', 'gy')), may hold values from 0 to 249
Outputs:
- core_grad: float32 [908800], P(('gx', 'gy'))
- top_grad: float32 [258, 256], replicated
Inputs may be any that keep to these rules, and one draw needn't show every extreme that they name: `bag_ids`: along a row, never falling; every sample of the block gets 1 to 8 lookups, one exactly 8.
All inputs are finite; a program needn't handle non-finite values. No bound on the sum of `labels` on one device may be relied on, other than what follows from the above.
Results may differ from a plain program's by a relative error of at most 0.0018.
The roundings to bfloat16 on the way count: a program that leaves them out, or rounds other values in their place, can miss the bound.
Values sent between devices are 32-bit elements; how exact they have to be, the bound alone decides.
A program may use at most 64 MiB of HBM per device.

v0:
```python
import functools
import types

import jax
import jax.numpy as jnp
from jax import lax
from jax.experimental import pallas as pl
from jax.experimental.pallas import tpu as pltpu
from jax.sharding import PartitionSpec as P

D1 = 4
D2 = 4
D3 = 8
R = 32
WIDTH = D1 * D2 * D3
PAIRS = D1 * D2
SIDE = D2 * R
LANES = 128
AXES = ("gx", "gy")
F32 = jnp.float32
BF16 = jnp.bfloat16
HIGH = lax.Precision.HIGHEST
PLAIN, ACROSS, DOWN = ((1,), (0,)), ((1,), (1,)), ((0,), (0,))


def dot(a, b, dims, precision=None):
    return lax.dot_general(
        a, b, (dims, ((), ())), precision=precision, preferred_element_type=F32
    )


def parts_of(x, count):
    parts = []
    for _ in range(count):
        part = x.astype(BF16)
        parts.append(part)
        x = x - part.astype(F32)
    return parts


def dot_parts(a, b, dims, count, wide):
    total = None
    for part in parts_of((a, b)[wide], count):
        term = dot(part, b, dims) if wide == 0 else dot(a, part, dims)
        total = term if total is None else total + term
    return total


def hot(row, count, kind):
    numbers = lax.broadcasted_iota(jnp.int32, (count, row.shape[1]), 0)
    return jnp.where(numbers == row, 1.0, 0.0).astype(kind)


def by_d3(last_t):
    size = R * D3
    to = lax.broadcasted_iota(jnp.int32, (size, size), 0)
    of = lax.broadcasted_iota(jnp.int32, (size, size), 1)
    turn = jnp.where(of == (to % R) * D3 + to // R, 1.0, 0.0).astype(BF16)
    return dot(turn, last_t, PLAIN)


def up(count, step):
    return -(-count // step) * step


def plan_of(nx, ny, shape_one, shape_two, shape_three, shape_top):
    cores = 2
    if nx % cores:
        return None
    chips, planes, devices = nx // cores, ny, nx * ny
    n1, n2, n3 = (s[0] * s[1] for s in (shape_one, shape_two, shape_three))
    total = n1 + n2 + n3
    if total % devices or shape_one[1] != LANES or n1 % LANES or shape_two[1] % LANES:
        return None
    if shape_three[1] != cores * LANES or shape_top[1] != cores * LANES or shape_top[0] % (8 * chips):
        return None
    share = total // devices
    row = shape_two[1]
    window = min(-(-share // row) + 1, shape_two[0])
    segs, offset = [None] * planes, 0
    for d in range(devices):
        lo, hi = d * share, (d + 1) * share
        has_first, has_last = lo < n1, hi > n1 + n2
        if not (has_first or has_last):
            continue
        if has_first and has_last or segs[d % planes] is not None:
            return None
        seg = types.SimpleNamespace(owner=d // planes, first=has_first)
        if has_first:
            seg.lo, seg.hi = lo // LANES, -(-min(hi, n1) // LANES)
            seg.rows = up(-(-(seg.hi - seg.lo) // (cores * chips)), 8)
        else:
            seg.lo = max(lo - n1 - n2, 0) // shape_three[1] // 8 * 8
            seg.hi = -(-(hi - n1 - n2) // shape_three[1])
            seg.rows = up(-(-(seg.hi - seg.lo) // chips), 8)
        segs[d % planes] = seg
    if any(seg is None for seg in segs):
        return None
    for seg in segs:
        seg.offset = offset
        offset += seg.rows
    return types.SimpleNamespace(
        nx=nx, ny=ny, cores=cores, chips=chips, planes=planes, share=share, window=window,
        row=row, n1=n1, segs=segs, srows=offset, smost=max(seg.rows for seg in segs),
        trows=shape_top[0] // chips + 8, n2_rows=shape_two[0], n3_rows=shape_three[0])


def pieces_of(seg, cores, chips, halves):
    for core in range(cores):
        for chip in range(chips):
            n = core * chips + chip if seg.first else chip
            lo = seg.lo + n * seg.rows
            hi = min(lo + seg.rows, seg.hi)
            if lo < hi:
                yield core, chip, lo, hi, 0 if seg.first else core


def grad_left_into(gleft_s, g_s, lastd_s):
    @pl.loop(0, PAIRS)
    def _(p):
        total = None
        for d in range(D3):
            term = g_s[pl.ds(p * D3 + d, 1), :] * lastd_s[d * R:(d + 1) * R, :]
            total = term if total is None else total + term
        gleft_s[pl.ds(pl.multiple_of(p * R, R), R), :] = total


STAGES = ("dz", "dx", "dc", "gz", "gx", "gc", "t0", "t1", "t2", "t3", "t4", "s0", "s1", "s2", "s3")


def stage_sizes(plan):
    cores, chips, planes = plan.cores, plan.chips, plan.planes
    gather = dict(z=planes, x=chips * planes, c=cores * planes)
    sizes = {kind + axis: size for kind in "dg" for axis, size in gather.items()}
    sizes.update(t0=cores, t1=chips, t2=planes, t3=chips, t4=cores,
                 s0=cores, s1=chips, s2=planes, s3=cores * chips)
    return [sizes[name] for name in STAGES]


def step_kernel(plan, *refs):
    inputs, refs = refs[:12], refs[12:]
    digits_ref, gp_ref, top_ref, seg_ref = refs[:4]
    held, refs = refs[4:16], refs[16:]
    mid_s, first_s, last_s, lastd_s, left_s, gleft_s, emb_s, g_s, gf_s, gl_s = refs[:10]
    top_s, topin, top1, topx, topz, seg_s, segin, seg1, segx, seg2, segz, seg3 = refs[10:22]
    load_sems, sems = refs[22], refs[23:]
    sems = {name: (sems[2 * i], sems[2 * i + 1]) for i, name in enumerate(STAGES)}
    cores, chips, planes = plan.cores, plan.chips, plan.planes
    gx, plane = lax.axis_index("gx"), lax.axis_index("gy")
    core, chip = gx % cores, gx // cores

    loads = [pltpu.make_async_copy(a, b, load_sems.at[k])
             for k, (a, b) in enumerate(zip(inputs, held))]
    for load in loads:
        load.start()

    def at(c, q, p):
        return (q * cores + c, p)

    def on_core(k):
        return at((core + k) % cores, chip, plane)

    def on_chip(k):
        return at(core, (chip + k) % chips, plane)

    def on_plane(k):
        return at(core, chip, (plane + k) % planes)

    barrier = pltpu.get_barrier_semaphore()
    peers = [at((core + c) % cores, (chip + q) % chips, plane)
             for c in range(cores) for q in range(chips) if c or q]
    peers += [on_plane(k) for k in range(1, planes)]
    for peer in peers:
        pl.semaphore_signal(barrier, inc=1, device_id=peer, device_id_type=pl.DeviceIdType.MESH)

    sent = []

    def remote(src, dst, stage, k, peer):
        return pltpu.make_async_remote_copy(
            src_ref=src, dst_ref=dst, send_sem=sems[stage][0].at[k],
            recv_sem=sems[stage][1].at[k], device_id=peer,
            device_id_type=pl.DeviceIdType.MESH)

    def push(src, dst, stage, k, peer):
        copy = remote(src, dst, stage, k, peer)
        copy.start()
        sent.append(copy)

    def arrive(ref, stage, k):
        remote(ref, ref, stage, k, on_plane(1)).wait_recv()

    def back(me, k, size):
        return (me + size - k) % size

    class Gather:
        def __init__(self, ref, kind):
            self.ref, self.kind = ref, kind

        def own(self):
            slot = self.ref.at[core, plane, chip]
            for k in range(1, planes):
                push(slot, slot, self.kind + "z", k, on_plane(k))
            for q in range(1, chips):
                push(slot, slot, self.kind + "x", q * planes, on_chip(q))

        def relay_z(self, k):
            slot = self.ref.at[core, back(plane, k, planes), chip]
            arrive(slot, self.kind + "z", k)
            for q in range(1, chips):
                push(slot, slot, self.kind + "x", q * planes + k, on_chip(q))

        def relay_x(self, k):
            z = back(plane, k, planes)
            for q in range(1, chips):
                arrive(self.ref.at[core, z, back(chip, q, chips)], self.kind + "x", q * planes + k)
            slot = self.ref.at[core, z]
            for c in range(1, cores):
                push(slot, slot, self.kind + "c", c * planes + k, on_core(c))

        def finish(self, k):
            for c in range(1, cores):
                slot = self.ref.at[back(core, c, cores), back(plane, k, planes)]
                arrive(slot, self.kind + "c", c * planes + k)

    digits, grads = Gather(digits_ref, "d"), Gather(gp_ref, "g")

    for load in loads:
        load.wait()
    c1, c2, c3, dense, w, bias, wout, labels, bag, d1, d2, d3 = held
    samples, looks = dense.shape[0], d1.shape[1]
    per = looks // LANES
    for k, digit in enumerate((bag, d1, d2, d3)):
        for h in range(per):
            digits_ref[core, plane, chip, k * per + h:k * per + h + 1, :] = (
                digit[:, h * LANES:(h + 1) * LANES].astype(F32))

    hot1 = hot(d1[...], c1.shape[0], BF16)
    hot2 = hot(d2[...], c2.shape[0], BF16)
    hot3 = hot(d3[...], c3.shape[0], BF16)
    for start in range(0, R * SIDE, 512):
        mid_s[start:start + 512, :] = dot(c2[:, start:start + 512], hot2, DOWN)
    first_s[...] = dot(c1[...], hot1, DOWN)
    last_t = dot(c3[...], hot3, DOWN)
    last_s[...] = last_t
    lastd_s[...] = by_d3(last_t.astype(BF16))

    pl.semaphore_wait(barrier, len(peers))
    digits.own()

    lane_blocks = looks // LANES

    @pl.loop(0, D2 * lane_blocks)
    def _(step):
        j = step // lane_blocks
        lanes = pl.ds(pl.multiple_of((step % lane_blocks) * LANES, LANES), LANES)
        totals = [None] * D1
        for a in range(R):
            m = mid_s[pl.ds(pl.multiple_of(a * SIDE + j * R, R), R), lanes]
            for i in range(D1):
                term = first_s[i * R + a:i * R + a + 1, lanes] * m
                totals[i] = term if totals[i] is None else totals[i] + term
        for i in range(D1):
            left_s[pl.ds(pl.multiple_of(i * SIDE + j * R, R), R), lanes] = totals[i]

    @pl.loop(0, PAIRS)
    def _(p):
        totals = [None, None]
        for c in range(R):
            term = left_s[pl.ds(p * R + c, 1), :] * last_s[c * D3:(c + 1) * D3, :]
            k = c % 2
            totals[k] = term if totals[k] is None else totals[k] + term
        emb_s[pl.ds(pl.multiple_of(p * D3, D3), D3), :] = totals[0] + totals[1]

    for k in range(1, planes):
        digits.relay_z(k)

    bags = hot(bag[...], samples, BF16)
    pooled = dot_parts(bags, emb_s[...], ACROSS, 3, 1).astype(BF16)
    pre = (
        dot(dense[...], w[:WIDTH, :], PLAIN) + dot(pooled, w[WIDTH:, :], PLAIN)
        + bias[...]
    )
    sig = jax.nn.sigmoid(pre)
    hidden = pre * sig
    logit = jnp.sum(hidden * wout[...], axis=1, keepdims=True)
    rows = lax.broadcasted_iota(jnp.int32, (samples, samples), 0)
    cols = lax.broadcasted_iota(jnp.int32, (samples, samples), 1)
    label = jnp.sum(
        jnp.where(rows == cols, labels[...].astype(F32), 0.0), axis=1, keepdims=True
    )
    dlogit = (jax.nn.sigmoid(logit) - label) / samples
    dpre = dlogit * wout[...] * (sig * (1.0 + pre * (1.0 - sig)))
    low = dpre.astype(BF16)
    gp = dot(low, w[WIDTH:, :], ACROSS)
    gp_ref[core, plane, chip] = gp
    grads.own()

    deep = plan.trows - 8
    vectors = jnp.concatenate(
        [jnp.sum(dpre, axis=0, keepdims=True), jnp.sum(hidden * dlogit, axis=0, keepdims=True),
         jnp.zeros((6, dpre.shape[1]), F32)], axis=0)
    weight = [dot(dense[...], low, DOWN), dot(pooled, low, DOWN)]
    for h in range(cores):
        lanes = slice(h * LANES, (h + 1) * LANES)
        for q in range(chips):
            lo = q * deep
            half = weight[lo // WIDTH]
            top_s[h, q, :deep, :] = half[lo % WIDTH:lo % WIDTH + deep, lanes]
            top_s[h, q, deep:, :] = vectors[:, lanes] if q == 0 else jnp.zeros((8, LANES), F32)
    for c in range(1, cores):
        push(top_s.at[(core + c) % cores], topin.at[c], "t0", c, on_core(c))

    g_s[...] = dot_parts(gp, bags, DOWN, 2, 0)
    grad_left_into(gleft_s, g_s, lastd_s)
    for k in range(planes):
        digits.relay_x(k)

    total = top_s[core]
    for c in range(1, cores):
        arrive(topin.at[c], "t0", c)
        total = total + topin[c]
    top1[...] = total
    for k in range(1, chips):
        push(top1.at[(chip + k) % chips], topx.at[k], "t1", k, on_chip(k))

    @pl.loop(0, R)
    def _(c):
        totals = [None, None]
        for p in range(PAIRS):
            term = left_s[pl.ds(p * R + c, 1), :] * g_s[p * D3:(p + 1) * D3, :]
            k = p % 2
            totals[k] = term if totals[k] is None else totals[k] + term
        gl_s[pl.ds(pl.multiple_of(c * D3, D3), D3), :] = totals[0] + totals[1]

    @pl.loop(0, R)
    def _(a):
        totals = [None] * D1
        for t in range(0, SIDE, 8):
            m = mid_s[pl.ds(pl.multiple_of(a * SIDE + t, 8), 8), :]
            for i in range(D1):
                term = gleft_s[i * SIDE + t:i * SIDE + t + 8, :] * m
                totals[i] = term if totals[i] is None else totals[i] + term
        for i in range(D1):
            gf_s[pl.ds(i * R + a, 1), :] = jnp.sum(totals[i], axis=0, keepdims=True)

    sums = {True: dot_parts(hot1, gf_s[...], ACROSS, 2, 1),
            False: dot_parts(hot3, gl_s[...], ACROSS, 2, 1)}
    seg_s[...] = jnp.zeros_like(seg_s)
    for seg in plan.segs:
        for c, q, lo, hi, h in pieces_of(seg, cores, chips, cores):
            seg_s[c, q, seg.offset:seg.offset + hi - lo, :] = (
                sums[seg.first][lo:hi, h * LANES:(h + 1) * LANES])
    for c in range(1, cores):
        push(seg_s.at[(core + c) % cores], segin.at[c], "s0", c, on_core(c))

    for k in range(1, planes):
        grads.relay_z(k)

    total = top1[chip]
    for k in range(1, chips):
        arrive(topx.at[k], "t1", k)
        total = total + topx[k]
    topz[plane] = total
    for k in range(1, planes):
        push(topz.at[plane], topz.at[plane], "t2", k, on_plane(k))

    total = seg_s[core]
    for c in range(1, cores):
        arrive(segin.at[c], "s0", c)
        total = total + segin[c]
    seg1[...] = total
    for k in range(1, chips):
        push(seg1.at[(chip + k) % chips], segx.at[k], "s1", k, on_chip(k))

    for k in range(planes):
        grads.relay_x(k)

    total = seg1[chip]
    for k in range(1, chips):
        arrive(segx.at[k], "s1", k)
        total = total + segx[k]
    seg2[...] = total

    def out_of(p, k):
        seg = plan.segs[(p + k) % planes]
        return remote(seg2.at[seg.offset:seg.offset + seg.rows],
                      segz.at[k, :seg.rows], "s2", k, on_plane(k))

    for p in range(planes):
        @pl.when(plane == p)
        def _(p=p):
            for k in range(1, planes):
                out_of(p, k).start()

    for k in range(1, planes):
        arrive(topz.at[back(plane, k, planes)], "t2", k)
    total = topz[0]
    for k in range(1, planes):
        total = total + topz[k]
    top_ref[core, chip] = total
    for k in range(1, chips):
        push(top_ref.at[core, chip], top_ref.at[core, chip], "t3", k, on_chip(k))

    def to_owner(p):
        seg = plan.segs[p]
        return remote(seg3.at[:seg.rows], seg_ref.at[core, chip, :seg.rows], "s3",
                      core * chips + chip, (seg.owner, plane))

    for p in range(planes):
        @pl.when(plane == p)
        def _(p=p):
            seg = plan.segs[p]
            total = seg2[seg.offset:seg.offset + seg.rows]
            for k in range(1, planes):
                arrive(segz.at[k, :seg.rows], "s2", k)
                total = total + segz[k, :seg.rows]
            seg3[:seg.rows] = total

            @pl.when(gx != seg.owner)
            def _():
                to_owner(p).start()

    for k in range(1, chips):
        arrive(top_ref.at[core, back(chip, k, chips)], "t3", k)
    for c in range(1, cores):
        push(top_ref.at[core], top_ref.at[core], "t4", c, on_core(c))

    for p in range(planes):
        seg = plan.segs[p]

        @pl.when((plane == p) & (gx == seg.owner))
        def _(p=p, seg=seg):
            own_core, own_chip = seg.owner % cores, seg.owner // cores
            seg_ref[own_core, own_chip, :seg.rows] = seg3[:seg.rows]
            for c in range(cores):
                for q in range(chips):
                    if (c, q) != (own_core, own_chip):
                        arrive(seg_ref.at[c, q, :seg.rows], "s3", c * chips + q)

    for k in range(planes):
        digits.finish(k)
        grads.finish(k)
    for c in range(1, cores):
        arrive(top_ref.at[back(core, c, cores)], "t4", c)
    for copy in sent:
        copy.wait_send()
    for p in range(planes):
        @pl.when(plane == p)
        def _(p=p):
            for k in range(1, planes):
                out_of(p, k).wait_send()

            @pl.when(gx != plan.segs[p].owner)
            def _():
                to_owner(p).wait_send()


def step_part(plan, *inputs):
    c1, c2, c3, dense, w, bias, wout, labels, bag, d1, d2, d3 = inputs
    samples, looks = dense.shape[0], d1.shape[1]
    cores, chips, planes = plan.cores, plan.chips, plan.planes
    shape = lambda *dims: jax.ShapeDtypeStruct(dims, F32)
    vmem = pl.BlockSpec(memory_space=pltpu.VMEM)
    scratch = [R * SIDE, D1 * R, R * D3, R * D3, D1 * SIDE, D1 * SIDE, WIDTH, WIDTH, D1 * R, R * D3]
    top, seg = (plan.trows, LANES), (plan.srows, LANES)
    sums = [
        (cores, chips, *top), (cores, chips, *top), (chips, *top), (chips, *top), (planes, *top),
        (cores, chips, *seg), (cores, chips, *seg), (chips, *seg), (chips, *seg), seg,
        (planes, plan.smost, LANES), (plan.smost, LANES)]
    return pl.pallas_call(
        functools.partial(step_kernel, plan),
        in_specs=[pl.BlockSpec(memory_space=pltpu.HBM)] * len(inputs),
        out_specs=(vmem,) * 4,
        out_shape=(
            shape(cores, planes, chips, up(4 * looks // LANES, 8), LANES),
            shape(cores, planes, chips, samples, WIDTH),
            shape(cores, chips, *top),
            shape(cores, chips, plan.smost, LANES),
        ),
        scratch_shapes=[pltpu.VMEM(x.shape, x.dtype) for x in inputs]
        + [pltpu.VMEM((rows, looks), F32) for rows in scratch]
        + [pltpu.VMEM(dims, F32) for dims in sums]
        + [pltpu.SemaphoreType.DMA((len(inputs),))]
        + [pltpu.SemaphoreType.DMA((size,)) for size in stage_sizes(plan) for _ in range(2)],
        compiler_params=pltpu.CompilerParams(
            collective_id=0, has_side_effects=True, vmem_limit_bytes=40 << 20),
        name="step",
    )(*inputs)


def finish_kernel(
    plan, chunk, c1, c3, digits_in, gp_in, top, seg_in, core_ref, top_ref,
    rank_s, vals_s, g_s, lastd_s, gleft_s, big_s,
):
    cores, chips, planes, window = plan.cores, plan.chips, plan.planes, plan.window
    gx, plane = lax.axis_index("gx"), lax.axis_index("gy")
    start = (gx * planes + plane) * plan.share
    r0 = jnp.clip((start - plan.n1) // plan.row, 0, plan.n2_rows - window)
    samples = gp_in.shape[3]
    groups = cores * planes * chips
    gp = gp_in[...].reshape(groups * samples, WIDTH)
    blocks = digits_in[...].reshape(groups, *digits_in.shape[3:])

    deep = plan.trows - 8
    for h in range(cores):
        lanes = slice(h * LANES, (h + 1) * LANES)
        for q in range(chips):
            top_ref[q * deep:(q + 1) * deep, lanes] = top[h, q, :deep, :]
        top_ref[chips * deep:, lanes] = top[h, 0, deep:deep + 2, :]

    looks = rank_s.shape[1]
    per = looks // LANES
    digits = [
        jnp.concatenate([blocks[:, k * per + h, :] for h in range(per)], axis=1).astype(jnp.int32)
        for k in range(4)
    ]
    rel = digits[2] - r0
    inside = (rel >= 0) & (rel < window)
    low = jnp.where(inside, 1.0, 0.0).astype(BF16)
    tri = jnp.where(
        lax.broadcasted_iota(jnp.int32, (looks, looks), 0)
        < lax.broadcasted_iota(jnp.int32, (looks, looks), 1), 1.0, 0.0).astype(BF16)
    above = jnp.where(
        lax.broadcasted_iota(jnp.int32, (groups, groups), 0)
        > lax.broadcasted_iota(jnp.int32, (groups, groups), 1), 1.0, 0.0).astype(BF16)
    before = jnp.sum(dot(above, low, PLAIN), axis=1, keepdims=True)
    rank_s[...] = jnp.where(inside, dot(low, tri, PLAIN) + before, -1.0).astype(jnp.int32)
    count = jnp.sum(jnp.where(inside, 1, 0))
    group = lax.broadcasted_iota(jnp.int32, (groups, looks), 0)
    columns = (digits[0], digits[1], digits[3], group, jnp.where(inside, rel + 1, 0))
    for k, column in enumerate(columns):
        vals_s[:, k:k + 1, :] = column.astype(F32).reshape(groups, 1, looks)
    vals_s[:, len(columns):, :] = jnp.zeros((groups, 8 - len(columns), looks), F32)
    base = plan.n1 // LANES
    rows = window * R
    big_s[base:base + rows, :] = jnp.zeros((rows, LANES), F32)
    gp_high, gp_low = parts_of(gp, 2)
    slots = lax.broadcasted_iota(jnp.int32, (chunk, looks), 0)

    def body(step, carry):
        def pick(e, found):
            ranks = rank_s[pl.ds(e, 1), :] - step * chunk
            chosen = jnp.where(slots == ranks, 1.0, 0.0).astype(BF16)
            return found + dot(vals_s[e].astype(BF16), chosen, ACROSS)

        found = lax.fori_loop(0, groups, pick, jnp.zeros((8, chunk), F32), unroll=4)
        found = found.astype(jnp.int32)
        bag, d1, d3, owner, rel1 = (found[k:k + 1, :] for k in range(5))
        first = dot(c1[...], hot(d1, c1.shape[0], BF16), DOWN)
        last = dot(c3[...], hot(d3, c3.shape[0], BF16), DOWN)
        lastd_s[...] = by_d3(last.astype(BF16))
        sample = hot(owner * samples + bag, gp.shape[0], BF16)
        g_s[...] = dot(gp_high, sample, DOWN) + dot(gp_low, sample, DOWN)
        grad_left_into(gleft_s, g_s, lastd_s)
        total = big_s[base:base + rows, :]
        for i in range(D1):
            part = first[i * R:(i + 1) * R, :]
            spread = jnp.concatenate(
                [jnp.where(rel1 == r + 1, part, 0.0) for r in range(window)], axis=0
            ).astype(BF16)
            total = total + dot_parts(spread, gleft_s[i * SIDE:(i + 1) * SIDE, :], ACROSS, 2, 1)
        big_s[base:base + rows, :] = total
        return carry

    lax.fori_loop(0, (count + chunk - 1) // chunk, body, 0)

    halves = seg_in.shape[0]
    for p in range(planes):
        seg = plan.segs[p]

        @pl.when((plane == p) & (gx == seg.owner))
        def _(seg=seg):
            for c, q, lo, hi, h in pieces_of(seg, cores, chips, halves):
                piece = seg_in[c, q, :hi - lo, :]
                if seg.first:
                    big_s[lo:hi, :] = piece
                else:
                    big_s[pl.ds(base + rows + lo * halves + h, hi - lo, stride=halves), :] = piece

    at = start // LANES - r0 * (plan.row // LANES)
    shift = start % LANES
    count = core_ref.shape[0]
    here, after = big_s[pl.ds(at, count), :], big_s[pl.ds(at + 1, count), :]
    turn = (LANES - shift) % LANES
    lane = lax.broadcasted_iota(jnp.int32, (count, LANES), 1)
    core_ref[...] = jnp.where(
        lane < LANES - shift, pltpu.roll(here, turn, 1), pltpu.roll(after, turn, 1))


def finish_part(plan, looks, c1, c3, digits, gp, top, seg):
    groups = plan.cores * plan.chips * plan.planes
    chunk = 512
    vmem = pl.BlockSpec(memory_space=pltpu.VMEM)
    last_rows = plan.n3_rows * seg.shape[0]
    out_rows = up(-(-plan.share // LANES), 8)
    big = up(plan.n1 // LANES + plan.window * R + last_rows + out_rows, 8)
    return pl.pallas_call(
        functools.partial(finish_kernel, plan, chunk),
        out_shape=(
            jax.ShapeDtypeStruct((out_rows, LANES), F32),
            jax.ShapeDtypeStruct((plan.chips * (plan.trows - 8) + 2, plan.cores * LANES), F32),
        ),
        in_specs=[vmem] * 6,
        out_specs=(vmem, vmem),
        scratch_shapes=[
            pltpu.VMEM((groups, looks), jnp.int32),
            pltpu.VMEM((groups, 8, looks), F32),
            pltpu.VMEM((WIDTH, chunk), F32),
            pltpu.VMEM((R * D3, chunk), F32),
            pltpu.VMEM((D1 * SIDE, chunk), F32),
            pltpu.VMEM((big, LANES), F32),
        ],
        compiler_params=pltpu.CompilerParams(vmem_limit_bytes=40 << 20),
        name="finish",
    )(c1, c3, digits, gp, top, seg)


def per_device(plan, c1, c2, c3, dense, w, bias, wout, labels, bag, d1, d2, d3):
    digits, gp, top, seg = step_part(
        plan, c1, c2, c3, dense, w, bias[None], wout[None], labels[None], bag, d1, d2, d3)
    core, top = finish_part(plan, d1.shape[1], c1, c3, digits, gp, top, seg)
    return core.reshape(-1)[:plan.share], top


def one_hot(digits, count, kind):
    return (digits[:, None] == jnp.arange(count, dtype=jnp.int32)[None, :]).astype(kind)


def slices(digits, core):
    return jnp.dot(
        one_hot(digits, core.shape[0], jnp.bfloat16), core, preferred_element_type=jnp.float32
    )


def factors(digits, cores):
    high = lax.Precision.HIGHEST
    first = slices(digits[0], cores[0]).reshape(-1, D1, R)
    middle = slices(digits[1], cores[1]).reshape(-1, R, D2 * R)
    last = slices(digits[2], cores[2]).reshape(-1, R, D3)
    left = jnp.einsum("nia,nab->nib", first, middle, precision=high).reshape(-1, D1 * D2, R)
    return (first, middle, last, left)


def top_total(top_local):
    return lax.psum(top_local, ("gx", "gy"))


def per_device_dense(
    core_one,
    core_two,
    core_three,
    dense_rows,
    w_top,
    bias_top,
    w_out,
    labels,
    bag_ids,
    digit_one,
    digit_two,
    digit_three,
):
    high = lax.Precision.HIGHEST
    cores = (core_one, core_two, core_three)
    digits = jnp.stack([digit_one[0], digit_two[0], digit_three[0]])
    looks = digits.shape[1]
    block = min(256, looks)
    blocks = looks // block
    blocked = digits.reshape(3, blocks, block).transpose(1, 0, 2)
    width = D1 * D2 * D3

    def forward(carry, part):
        first, middle, last, left = factors(part, cores)
        return (carry, jnp.einsum("npa,nad->npd", left, last, precision=high).reshape(block, width))

    _, embedded = lax.scan(forward, jnp.zeros((), jnp.float32), blocked)
    embedded = embedded.reshape(looks, width)
    samples = dense_rows.shape[0]
    bag_table = one_hot(bag_ids[0], samples, jnp.float32)
    pooled = jnp.dot(bag_table.T, embedded, precision=high)
    joined = jnp.concatenate([dense_rows, pooled.astype(jnp.bfloat16)], axis=1)
    pre = jnp.dot(joined, w_top, preferred_element_type=jnp.float32) + bias_top[None, :]
    sig = jax.nn.sigmoid(pre)
    hidden = pre * sig
    logit = jnp.dot(hidden, w_out, precision=high)
    dlogit = (jax.nn.sigmoid(logit) - labels.astype(jnp.float32)) / samples
    dpre = dlogit[:, None] * w_out[None, :] * (sig * (1.0 + pre * (1.0 - sig)))
    dpre_low = dpre.astype(jnp.bfloat16)
    grad_weight = jnp.dot(joined.T, dpre_low, preferred_element_type=jnp.float32)
    grad_bias = jnp.sum(dpre, axis=0)
    grad_output = jnp.sum(hidden * dlogit[:, None], axis=0)
    top_local = jnp.concatenate([grad_weight, grad_bias[None, :], grad_output[None, :]], axis=0)
    grad_pooled = jnp.dot(dpre_low, w_top[width:].T, preferred_element_type=jnp.float32)
    grad_embedded = jnp.dot(bag_table, grad_pooled, precision=high).reshape(blocks, block, width)

    def backward(totals, inputs):
        part, grad_block = inputs
        first, middle, last, left = factors(part, cores)
        grad_view = grad_block.reshape(block, D1 * D2, D3)
        grad_last = jnp.einsum("npa,npd->nad", left, grad_view, precision=high)
        grad_left = jnp.einsum("npd,nad->npa", grad_view, last, precision=high).reshape(
            block, D1, D2 * R
        )
        grad_first = jnp.einsum("nib,nab->nia", grad_left, middle, precision=high)
        grad_middle = jnp.einsum("nia,nib->nab", first, grad_left, precision=high)
        pieces = (
            grad_first.reshape(block, -1),
            grad_middle.reshape(block, -1),
            grad_last.reshape(block, -1),
        )
        updated = tuple(
            (
                total
                + jnp.dot(
                    one_hot(part[number], cores[number].shape[0], jnp.float32).T,
                    pieces[number],
                    precision=high,
                )
                for number, total in enumerate(totals)
            )
        )
        return (updated, None)

    start = tuple((jnp.zeros(core.shape, jnp.float32) for core in cores))
    totals, _ = lax.scan(backward, start, (blocked, grad_embedded))
    flat = jnp.concatenate([total.reshape(-1) for total in totals])
    core_grad = lax.psum_scatter(flat, ("gx", "gy"), scatter_dimension=0, tiled=True)
    top_grad = top_total(top_local)
    return (core_grad, top_grad)


def solution(mesh):
    nx, ny = mesh.shape["gx"], mesh.shape["gy"]
    whole, split, rows = P(), P(AXES), P(AXES, None)

    def step(*args):
        cores, dense = args[:3], args[3]
        plan = None
        if dense.size < sum(core.size for core in cores):
            plan = plan_of(nx, ny, *(core.shape for core in cores), args[4].shape)
        body = functools.partial(per_device, plan) if plan else per_device_dense
        return jax.shard_map(
            body,
            mesh=mesh,
            in_specs=(
                whole, whole, whole, rows, whole, whole, whole, split,
                rows, rows, rows, rows,
            ),
            out_specs=(split, whole),
            check_vma=False,
        )(*args)

    return step
```

profile of v0, /device:TPU:0, one launch (start us, length us, event | category | flops | bytes accessed | tf_op | source)
XLA Modules:
  0.0 50.0 jit_solution(14987369080281808664)
XLA Ops:
  0.6 0.0 copy-start
  0.6 1.4 %copy-done = bf16[200,4096]{1,0:T(8,128)(2,1)S(1)} copy-done((bf16[200,4096]{1,0:T(8,128)(2,1)S(1)}, bf16[200,4096]{1,0:T(8,128)(2,1)}, u32[]{:S(2)}) %copy-start) | copy-done | bytes 1638424
  2.1 0.0 copy-start.1
  2.1 0.9 %copy-done.1 = bf16[250,256]{1,0:T(8,128)(2,1)S(1)} copy-done((bf16[250,256]{1,0:T(8,128)(2,1)S(1)}, bf16[250,256]{1,0:T(8,128)(2,1)}, u32[]{:S(2)}) %copy-start.1) | copy-done | bytes 128024
  3.0 0.0 copy-start.3
  3.0 0.8 %copy-done.3 = bf16[200,128]{1,0:T(8,128)(2,1)S(1)} copy-done((bf16[200,128]{1,0:T(8,128)(2,1)S(1)}, bf16[200,128]{1,0:T(8,128)(2,1)}, u32[]{:S(2)}) %copy-start.3) | copy-done | bytes 51224
  3.8 0.0 copy-start.4
  3.8 0.9 %copy-done.4 = bf16[256,256]{1,0:T(8,128)(2,1)S(1)} copy-done((bf16[256,256]{1,0:T(8,128)(2,1)S(1)}, bf16[256,256]{1,0:T(8,128)(2,1)}, u32[]{:S(2)}) %copy-start.4) | copy-done | bytes 131096
  4.7 0.0 copy-start.5
  4.7 0.7 %copy-done.5 = bf16[64,128]{1,0:T(8,128)(2,1)S(1)} copy-done((bf16[64,128]{1,0:T(8,128)(2,1)S(1)}, bf16[64,128]{1,0:T(8,128)(2,1)}, u32[]{:S(2)}) %copy-start.5) | copy-done | bytes 16408
  5.4 0.0 copy-start.6
  5.4 0.7 %copy-done.6 = f32[256]{0:T(256)S(1)} copy-done((f32[256]{0:T(256)S(1)}, f32[256]{0:T(256)}, u32[]{:S(2)}) %copy-start.6) | copy-done | bytes 1048
  6.1 0.0 copy-start.7
  6.1 0.7 %copy-done.7 = f32[256]{0:T(256)S(1)} copy-done((f32[256]{0:T(256)S(1)}, f32[256]{0:T(256)}, u32[]{:S(2)}) %copy-start.7) | copy-done | bytes 1048
  6.8 0.0 copy-start.8
  6.8 0.7 %copy-done.8 = s32[1,256]{1,0:T(1,128)S(1)} copy-done((s32[1,256]{1,0:T(1,128)S(1)}, s32[1,256]{1,0:T(1,128)}, u32[]{:S(2)}) %copy-start.8) | copy-done | bytes 1048
  7.4 0.0 copy-start.9
  7.4 0.7 %copy-done.9 = s32[1,256]{1,0:T(1,128)S(1)} copy-done((s32[1,256]{1,0:T(1,128)S(1)}, s32[1,256]{1,0:T(1,128)}, u32[]{:S(2)}) %copy-start.9) | copy-done | bytes 1048
  8.1 0.0 copy-start.10
  8.1 0.7 %copy-done.10 = s32[1,256]{1,0:T(1,128)S(1)} copy-done((s32[1,256]{1,0:T(1,128)S(1)}, s32[1,256]{1,0:T(1,128)}, u32[]{:S(2)}) %copy-start.10) | copy-done | bytes 1048
  8.8 0.0 copy-start.11
  8.8 0.7 %copy-done.11 = s32[1,256]{1,0:T(1,128)S(1)} copy-done((s32[1,256]{1,0:T(1,128)S(1)}, s32[1,256]{1,0:T(1,128)}, u32[]{:S(2)}) %copy-start.11) | copy-done | bytes 1048
  9.5 0.0 copy-start.12
  9.5 0.7 %copy-done.12 = s32[64]{0:T(128)S(1)} copy-done((s32[64]{0:T(128)S(1)}, s32[64]{0:T(128)}, u32[]{:S(2)}) %copy-start.12) | copy-done | bytes 280
  10.1 0.0 copy-start.2
  10.1 32.7 %step.1 = (f32[2,4,4,8,128]{4,3,2,1,0:T(8,128)S(1)}, f32[2,4,4,64,128]{4,3,2,1,0:T(8,128)S(1)}, f32[2,4,72,128]{3,2,1,0:T(8,128)S(1)}, f32[2,4,32,128]{3,2,1,0:T(8,128)S(1)}) custom-call(bf16[200,128]{1,0:T(8,128)(2,1)S(1)} %copy-done.3, bf16[200,4096]{1,0:T(8,128)(2,1)S(1)} %copy-done, bf16[250,256]{1,0:T(8,128)(2,1)S(1)} %copy-done.1, ...), custom_call_target="tpu_custom_call" | custom-call | tf_op jit(solution)/shard_map/step/pallas_call | solution.py:470
  42.8 0.0 copy-done.2
  42.8 7.2 %finish.1 = (f32[224,128]{1,0:T(8,128)}, f32[258,256]{1,0:T(8,128)}) custom-call(bf16[200,128]{1,0:T(8,128)(2,1)S(1)} %copy-done.3, bf16[250,256]{1,0:T(8,128)(2,1)S(1)} %copy-done.2, f32[2,4,4,8,128]{4,3,2,1,0:T(8,128)S(1)} %get-tuple-element.8.digits_in, f32[2,4,4,64,128]{4,3,2,1,0:T(8,128)S(1)} %get-tuple-element.9.gp_in, ...), custom_call_target="tpu_custom_call" | custom-call | tf_op jit(solution)/shard_map/finish/pallas_call | solution.py:597
Async XLA Ops:
  0.6 1.4 %copy-start = (bf16[200,4096]{1,0:T(8,128)(2,1)S(1)}, bf16[200,4096]{1,0:T(8,128)(2,1)}, u32[]{:S(2)}) copy-start(bf16[200,4096]{1,0:T(8,128)(2,1)} %refs_1_.1) | copy-start | bytes 4915204
  2.1 0.9 %copy-start.1 = (bf16[250,256]{1,0:T(8,128)(2,1)S(1)}, bf16[250,256]{1,0:T(8,128)(2,1)}, u32[]{:S(2)}) copy-start(bf16[250,256]{1,0:T(8,128)(2,1)} %c3.1) | copy-start | bytes 384004
  3.0 0.8 %copy-start.3 = (bf16[200,128]{1,0:T(8,128)(2,1)S(1)}, bf16[200,128]{1,0:T(8,128)(2,1)}, u32[]{:S(2)}) copy-start(bf16[200,128]{1,0:T(8,128)(2,1)} %c1.1) | copy-start | bytes 153604
  3.8 0.9 %copy-start.4 = (bf16[256,256]{1,0:T(8,128)(2,1)S(1)}, bf16[256,256]{1,0:T(8,128)(2,1)}, u32[]{:S(2)}) copy-start(bf16[256,256]{1,0:T(8,128)(2,1)} %refs_4_.1) | copy-start | bytes 393220
  4.7 0.7 %copy-start.5 = (bf16[64,128]{1,0:T(8,128)(2,1)S(1)}, bf16[64,128]{1,0:T(8,128)(2,1)}, u32[]{:S(2)}) copy-start(bf16[64,128]{1,0:T(8,128)(2,1)} %refs_3_.1) | copy-start | bytes 49156
  5.4 0.7 %copy-start.6 = (f32[256]{0:T(256)S(1)}, f32[256]{0:T(256)}, u32[]{:S(2)}) copy-start(f32[256]{0:T(256)} %param.17) | copy-start | bytes 3076
  6.1 0.7 %copy-start.7 = (f32[256]{0:T(256)S(1)}, f32[256]{0:T(256)}, u32[]{:S(2)}) copy-start(f32[256]{0:T(256)} %param.18) | copy-start | bytes 3076
  6.8 0.7 %copy-start.8 = (s32[1,256]{1,0:T(1,128)S(1)}, s32[1,256]{1,0:T(1,128)}, u32[]{:S(2)}) copy-start(s32[1,256]{1,0:T(1,128)} %refs_8_.1) | copy-start | bytes 3076
  7.4 0.7 %copy-start.9 = (s32[1,256]{1,0:T(1,128)S(1)}, s32[1,256]{1,0:T(1,128)}, u32[]{:S(2)}) copy-start(s32[1,256]{1,0:T(1,128)} %refs_9_.1) | copy-start | bytes 3076
  8.1 0.7 %copy-start.10 = (s32[1,256]{1,0:T(1,128)S(1)}, s32[1,256]{1,0:T(1,128)}, u32[]{:S(2)}) copy-start(s32[1,256]{1,0:T(1,128)} %refs_10_.1) | copy-start | bytes 3076
  8.8 0.7 %copy-start.11 = (s32[1,256]{1,0:T(1,128)S(1)}, s32[1,256]{1,0:T(1,128)}, u32[]{:S(2)}) copy-start(s32[1,256]{1,0:T(1,128)} %refs_11_.1) | copy-start | bytes 3076
  9.5 0.7 %copy-start.12 = (s32[64]{0:T(128)S(1)}, s32[64]{0:T(128)}, u32[]{:S(2)}) copy-start(s32[64]{0:T(128)} %param.19) | copy-start | bytes 772
  10.1 32.7 %copy-start.2 = (bf16[250,256]{1,0:T(8,128)(2,1)S(1)}, bf16[250,256]{1,0:T(8,128)(2,1)}, u32[]{:S(2)}) copy-start(bf16[250,256]{1,0:T(8,128)(2,1)} %c3.1) | copy-start | bytes 384004
where the time goes:
time: 50.4 us; the launch traced here: 50 us
  Pallas kernels  39.8 us (79%)
  local copies, waits for them, and re-layouts  9.48 us (19%)
  between operations  0.67 us (1%)
    pallas_call x1, Pallas kernels, step_part(): pl.pallas_call(functools.partial(step_kernel, plan), in_specs=[pl.BlockSp...  32.7 us
    unnamed x26, local copies, waits for them, and re-layouts  9.48 us
    pallas_call x1, Pallas kernels, finish_part(): pl.pallas_call(functools.partial(finish_kernel, plan, chunk), out_shape=(...  7.17 us

commit v1 on v0

--- a/solution.py
+++ b/solution.py
@@ -115,14 +115,168 @@
                 yield core, chip, lo, hi, 0 if seg.first else core
 
 
+def spans(count, step):
+    return [(lo, min(step, count - lo)) for lo in range(0, count, step)]
+
+
+def lane_loop(count, lanes, body):
+    blocks = lanes // LANES
+
+    @pl.loop(0, count * blocks)
+    def _(step):
+        body(step // blocks, pl.ds(pl.multiple_of((step % blocks) * LANES, LANES), LANES))
+
+
+def add(total, term):
+    return term if total is None else total + term
+
+
+def left_into(left_s, first_s, mid_s):
+    def body(j, lanes):
+        totals = [None] * D1
+        for a in range(R):
+            m = mid_s[pl.ds(pl.multiple_of(a * SIDE + j * R, R), R), lanes]
+            for i in range(D1):
+                totals[i] = add(totals[i], first_s[i * R + a:i * R + a + 1, lanes] * m)
+        for i in range(D1):
+            left_s[pl.ds(pl.multiple_of(i * SIDE + j * R, R), R), lanes] = totals[i]
+
+    lane_loop(D2, left_s.shape[1], body)
+
+
+def embedded_into(emb_s, left_s, last_s, batch=8):
+    @pl.loop(0, PAIRS // batch)
+    def _(b):
+        totals = [None] * batch
+        for c in range(R):
+            last = last_s[c * D3:(c + 1) * D3, :]
+            for k in range(batch):
+                totals[k] = add(totals[k], left_s[pl.ds((b * batch + k) * R + c, 1), :] * last)
+        for k in range(batch):
+            emb_s[pl.ds(pl.multiple_of((b * batch + k) * D3, D3), D3), :] = totals[k]
+
+
 def grad_left_into(gleft_s, g_s, lastd_s):
-    @pl.loop(0, PAIRS)
-    def _(p):
-        total = None
+    batch = 4 if gleft_s.shape[1] <= 2 * LANES else 2
+
+    @pl.loop(0, PAIRS // batch)
+    def _(b):
+        totals = [None] * batch
         for d in range(D3):
-            term = g_s[pl.ds(p * D3 + d, 1), :] * lastd_s[d * R:(d + 1) * R, :]
-            total = term if total is None else total + term
-        gleft_s[pl.ds(pl.multiple_of(p * R, R), R), :] = total
+            last = lastd_s[d * R:(d + 1) * R, :]
+            for k in range(batch):
+                totals[k] = add(totals[k], g_s[pl.ds((b * batch + k) * D3 + d, 1), :] * last)
+        for k in range(batch):
+            gleft_s[pl.ds(pl.multiple_of((b * batch + k) * R, R), R), :] = totals[k]
+
+
+def grad_last_into(gl_s, left_s, g_s, batch=8):
+    @pl.loop(0, R // batch)
+    def _(b):
+        totals = [None] * batch
+        for p in range(PAIRS):
+            g = g_s[p * D3:(p + 1) * D3, :]
+            for k in range(batch):
+                totals[k] = add(totals[k], left_s[pl.ds(p * R + b * batch + k, 1), :] * g)
+        for k in range(batch):
+            gl_s[pl.ds(pl.multiple_of((b * batch + k) * D3, D3), D3), :] = totals[k]
+
+
+def grad_first_into(gf_s, gleft_s, mid_s, batch=8):
+    def body(b, lanes):
+        totals = [[None] * D1 for _ in range(batch)]
+        for t in range(0, SIDE, 8):
+            gleft = [gleft_s[i * SIDE + t:i * SIDE + t + 8, lanes] for i in range(D1)]
+            for k in range(batch):
+                at = pl.multiple_of((b * batch + k) * SIDE + t, 8)
+                m = mid_s[pl.ds(at, 8), lanes]
+                for i in range(D1):
+                    totals[k][i] = add(totals[k][i], gleft[i] * m)
+        for i in range(D1):
+            rows = [jnp.sum(totals[k][i], axis=0, keepdims=True) for k in range(batch)]
+            gf_s[pl.ds(pl.multiple_of(i * R + b * batch, 8), batch), lanes] = (
+                jnp.concatenate(rows, axis=0))
+
+    lane_loop(R // batch, gf_s.shape[1], body)
+
+
+def first_row(plan):
+    start = (lax.axis_index("gx") * plan.planes + lax.axis_index("gy")) * plan.share
+    return jnp.clip((start - plan.n1) // plan.row, 0, plan.n2_rows - plan.window), start
+
+
+def rank_lookups(plan, blocks, rank_s, vals_s):
+    groups, looks = rank_s.shape
+    per = looks // LANES
+    r0, _ = first_row(plan)
+    digits = [
+        jnp.concatenate([blocks[:, k * per + h, :] for h in range(per)], axis=1).astype(jnp.int32)
+        for k in range(4)
+    ]
+    rel = digits[2] - r0
+    inside = (rel >= 0) & (rel < plan.window)
+    low = jnp.where(inside, 1.0, 0.0).astype(BF16)
+    tri = jnp.where(
+        lax.broadcasted_iota(jnp.int32, (looks, looks), 0)
+        < lax.broadcasted_iota(jnp.int32, (looks, looks), 1), 1.0, 0.0).astype(BF16)
+    above = jnp.where(
+        lax.broadcasted_iota(jnp.int32, (groups, groups), 0)
+        > lax.broadcasted_iota(jnp.int32, (groups, groups), 1), 1.0, 0.0).astype(BF16)
+    before = jnp.sum(dot(above, low, PLAIN), axis=1, keepdims=True)
+    rank_s[...] = jnp.where(inside, dot(low, tri, PLAIN) + before, -1.0).astype(jnp.int32)
+    group = lax.broadcasted_iota(jnp.int32, (groups, looks), 0)
+    columns = (digits[0], digits[1], digits[3], group, jnp.where(inside, rel + 1, 0))
+    for k, column in enumerate(columns):
+        vals_s[:, k:k + 1, :] = column.astype(F32).reshape(groups, 1, looks)
+    vals_s[:, len(columns):, :] = jnp.zeros((groups, 8 - len(columns), looks), F32)
+    return jnp.sum(jnp.where(inside, 1.0, 0.0), axis=(0, 1), keepdims=True)
+
+
+def pick_into(found_s, step, rank_s, vals_s):
+    chunk = found_s.shape[1]
+    groups, looks = rank_s.shape
+    slots = lax.broadcasted_iota(jnp.int32, (chunk, looks), 0)
+
+    def pick(e, found):
+        ranks = rank_s[pl.ds(e, 1), :] - step * chunk
+        chosen = jnp.where(slots == ranks, 1.0, 0.0).astype(BF16)
+        return found + dot(vals_s[e].astype(BF16), chosen, ACROSS)
+
+    found = lax.fori_loop(0, groups, pick, jnp.zeros(found_s.shape, F32), unroll=4)
+    found_s[...] = found.astype(jnp.int32)
+
+
+def factors_into(fsel_s, lsel_s, found_s, c1, c3):
+    fsel_s[...] = dot(c1[...], hot(found_s[1:2, :], c1.shape[0], BF16), DOWN)
+    last = dot(c3[...], hot(found_s[2:3, :], c3.shape[0], BF16), DOWN)
+    lsel_s[...] = by_d3(last.astype(BF16))
+
+
+def middle_sum(plan, gp, samples, found_s, fsel_s, lsel_s, gsel_s, glsel_s):
+    sample = hot(found_s[3:4, :] * samples + found_s[0:1, :], gp.shape[0], BF16)
+    gsel_s[...] = dot_parts(gp, sample, DOWN, 2, 0)
+    grad_left_into(glsel_s, gsel_s, lsel_s)
+    rel1 = found_s[4:5, :]
+    total = None
+    for i in range(D1):
+        part = fsel_s[i * R:(i + 1) * R, :]
+        spread = jnp.concatenate(
+            [jnp.where(rel1 == r + 1, part, 0.0) for r in range(plan.window)], axis=0
+        ).astype(BF16)
+        total = add(total, dot_parts(spread, glsel_s[i * SIDE:(i + 1) * SIDE, :], ACROSS, 2, 1))
+    return total
+
+
+def select_scratch(groups, looks, chunk):
+    return [
+        pltpu.VMEM((groups, looks), jnp.int32),
+        pltpu.VMEM((groups, 8, looks), F32),
+        pltpu.VMEM((8, chunk), jnp.int32),
+        pltpu.VMEM((D1 * R, chunk), F32),
+        pltpu.VMEM((R * D3, chunk), F32),
+        pltpu.VMEM((WIDTH, chunk), F32),
+        pltpu.VMEM((D1 * SIDE, chunk), F32),
+    ]
 
 
 STAGES = ("dz", "dx", "dc", "gz", "gx", "gc", "t0", "t1", "t2", "t3", "t4", "s0", "s1", "s2", "s3")
@@ -139,20 +293,44 @@
 
 def step_kernel(plan, *refs):
     inputs, refs = refs[:12], refs[12:]
-    digits_ref, gp_ref, top_ref, seg_ref = refs[:4]
-    held, refs = refs[4:16], refs[16:]
+    digits_out, gp_out, top_ref, seg_ref, mid_ref, count_ref = refs[:6]
+    held, refs = refs[6:18], refs[18:]
     mid_s, first_s, last_s, lastd_s, left_s, gleft_s, emb_s, g_s, gf_s, gl_s = refs[:10]
-    top_s, topin, top1, topx, topz, seg_s, segin, seg1, segx, seg2, segz, seg3 = refs[10:22]
-    load_sems, sems = refs[22], refs[23:]
+    digits_ref, gp_ref = refs[10:12]
+    top_s, topin, top1, topx, topz, seg_s, segin, seg1, segx, seg2, segz, seg3 = refs[12:24]
+    rank_s, vals_s, found_s, fsel_s, lsel_s, gsel_s, glsel_s = refs[24:31]
+    load_sems, save_sems, sems = refs[31], refs[32], refs[33:]
     sems = {name: (sems[2 * i], sems[2 * i + 1]) for i, name in enumerate(STAGES)}
     cores, chips, planes = plan.cores, plan.chips, plan.planes
     gx, plane = lax.axis_index("gx"), lax.axis_index("gy")
     core, chip = gx % cores, gx // cores
-
-    loads = [pltpu.make_async_copy(a, b, load_sems.at[k])
-             for k, (a, b) in enumerate(zip(inputs, held))]
-    for load in loads:
-        load.start()
+    scopes = []
+
+    def mark(name):
+        if scopes:
+            scopes.pop().__exit__(None, None, None)
+        if name:
+            scopes.append(jax.named_scope(name))
+            scopes[-1].__enter__()
+
+    mark("m_start")
+    c1, c2, c3, dense, w, bias, wout, labels, bag, d1, d2, d3 = held
+    wide = c2.shape[1] // 4
+    loads = {}
+
+    def load(k, columns=None):
+        src, dst = inputs[k], held[k]
+        if columns is not None:
+            src, dst = src.at[:, columns], dst.at[:, columns]
+        n = len(loads)
+        loads[n] = pltpu.make_async_copy(src, dst, load_sems.at[n])
+        loads[n].start()
+        return n
+
+    early = [load(k) for k in (10, 9, 11, 8)]
+    tables = [load(1, slice(lo, lo + wide)) for lo in range(0, c2.shape[1], wide)]
+    early += [load(0)]
+    late = [load(k) for k in (2, 3, 4, 5, 6, 7)]
 
     def at(c, q, p):
         return (q * cores + c, p)
@@ -196,10 +374,13 @@
         def __init__(self, ref, kind):
             self.ref, self.kind = ref, kind
 
-        def own(self):
+        def own_z(self):
             slot = self.ref.at[core, plane, chip]
             for k in range(1, planes):
                 push(slot, slot, self.kind + "z", k, on_plane(k))
+
+        def own_x(self):
+            slot = self.ref.at[core, plane, chip]
             for q in range(1, chips):
                 push(slot, slot, self.kind + "x", q * planes, on_chip(q))
 
@@ -224,56 +405,39 @@
 
     digits, grads = Gather(digits_ref, "d"), Gather(gp_ref, "g")
 
-    for load in loads:
-        load.wait()
-    c1, c2, c3, dense, w, bias, wout, labels, bag, d1, d2, d3 = held
+    mark("m_gather")
+    for n in early:
+        loads[n].wait()
     samples, looks = dense.shape[0], d1.shape[1]
     per = looks // LANES
     for k, digit in enumerate((bag, d1, d2, d3)):
         for h in range(per):
             digits_ref[core, plane, chip, k * per + h:k * per + h + 1, :] = (
                 digit[:, h * LANES:(h + 1) * LANES].astype(F32))
-
     hot1 = hot(d1[...], c1.shape[0], BF16)
     hot2 = hot(d2[...], c2.shape[0], BF16)
+    first_s[...] = dot(c1[...], hot1, DOWN)
+    for k, n in enumerate(tables):
+        loads[n].wait()
+        for lo, size in spans(wide, 512):
+            lo += k * wide
+            mid_s[lo:lo + size, :] = dot(c2[:, lo:lo + size], hot2, DOWN)
+    mark("m_left")
+    left_into(left_s, first_s, mid_s)
+    for n in late:
+        loads[n].wait()
     hot3 = hot(d3[...], c3.shape[0], BF16)
-    for start in range(0, R * SIDE, 512):
-        mid_s[start:start + 512, :] = dot(c2[:, start:start + 512], hot2, DOWN)
-    first_s[...] = dot(c1[...], hot1, DOWN)
     last_t = dot(c3[...], hot3, DOWN)
     last_s[...] = last_t
     lastd_s[...] = by_d3(last_t.astype(BF16))
-
+    mark("m_barrier")
     pl.semaphore_wait(barrier, len(peers))
-    digits.own()
-
-    lane_blocks = looks // LANES
-
-    @pl.loop(0, D2 * lane_blocks)
-    def _(step):
-        j = step // lane_blocks
-        lanes = pl.ds(pl.multiple_of((step % lane_blocks) * LANES, LANES), LANES)
-        totals = [None] * D1
-        for a in range(R):
-            m = mid_s[pl.ds(pl.multiple_of(a * SIDE + j * R, R), R), lanes]
-            for i in range(D1):
-                term = first_s[i * R + a:i * R + a + 1, lanes] * m
-                totals[i] = term if totals[i] is None else totals[i] + term
-        for i in range(D1):
-            left_s[pl.ds(pl.multiple_of(i * SIDE + j * R, R), R), lanes] = totals[i]
-
-    @pl.loop(0, PAIRS)
-    def _(p):
-        totals = [None, None]
-        for c in range(R):
-            term = left_s[pl.ds(p * R + c, 1), :] * last_s[c * D3:(c + 1) * D3, :]
-            k = c % 2
-            totals[k] = term if totals[k] is None else totals[k] + term
-        emb_s[pl.ds(pl.multiple_of(p * D3, D3), D3), :] = totals[0] + totals[1]
-
-    for k in range(1, planes):
-        digits.relay_z(k)
-
+    digits.own_z()
+    digits.own_x()
+    mark("m_emb")
+    embedded_into(emb_s, left_s, last_s)
+
+    mark("m_top")
     bags = hot(bag[...], samples, BF16)
     pooled = dot_parts(bags, emb_s[...], ACROSS, 3, 1).astype(BF16)
     pre = (
@@ -291,10 +455,8 @@
     dlogit = (jax.nn.sigmoid(logit) - label) / samples
     dpre = dlogit * wout[...] * (sig * (1.0 + pre * (1.0 - sig)))
     low = dpre.astype(BF16)
-    gp = dot(low, w[WIDTH:, :], ACROSS)
-    gp_ref[core, plane, chip] = gp
-    grads.own()
-
+
+    mark("m_topgrad")
     deep = plan.trows - 8
     vectors = jnp.concatenate(
         [jnp.sum(dpre, axis=0, keepdims=True), jnp.sum(hidden * dlogit, axis=0, keepdims=True),
@@ -309,12 +471,15 @@
             top_s[h, q, deep:, :] = vectors[:, lanes] if q == 0 else jnp.zeros((8, LANES), F32)
     for c in range(1, cores):
         push(top_s.at[(core + c) % cores], topin.at[c], "t0", c, on_core(c))
-
+    gp = dot(low, w[WIDTH:, :], ACROSS)
+    gp_ref[core, plane, chip] = gp
+    grads.own_z()
+
+    mark("m_gleft")
     g_s[...] = dot_parts(gp, bags, DOWN, 2, 0)
     grad_left_into(gleft_s, g_s, lastd_s)
-    for k in range(planes):
-        digits.relay_x(k)
-
+
+    mark("m_t0")
     total = top_s[core]
     for c in range(1, cores):
         arrive(topin.at[c], "t0", c)
@@ -322,27 +487,16 @@
     top1[...] = total
     for k in range(1, chips):
         push(top1.at[(chip + k) % chips], topx.at[k], "t1", k, on_chip(k))
-
-    @pl.loop(0, R)
-    def _(c):
-        totals = [None, None]
-        for p in range(PAIRS):
-            term = left_s[pl.ds(p * R + c, 1), :] * g_s[p * D3:(p + 1) * D3, :]
-            k = p % 2
-            totals[k] = term if totals[k] is None else totals[k] + term
-        gl_s[pl.ds(pl.multiple_of(c * D3, D3), D3), :] = totals[0] + totals[1]
-
-    @pl.loop(0, R)
-    def _(a):
-        totals = [None] * D1
-        for t in range(0, SIDE, 8):
-            m = mid_s[pl.ds(pl.multiple_of(a * SIDE + t, 8), 8), :]
-            for i in range(D1):
-                term = gleft_s[i * SIDE + t:i * SIDE + t + 8, :] * m
-                totals[i] = term if totals[i] is None else totals[i] + term
-        for i in range(D1):
-            gf_s[pl.ds(i * R + a, 1), :] = jnp.sum(totals[i], axis=0, keepdims=True)
-
+    grads.own_x()
+
+    mark("m_gl")
+    grad_last_into(gl_s, left_s, g_s)
+    mark("m_dz")
+    for k in range(1, planes):
+        digits.relay_z(k)
+    mark("m_gf")
+    grad_first_into(gf_s, gleft_s, mid_s)
+    mark("m_segdot")
     sums = {True: dot_parts(hot1, gf_s[...], ACROSS, 2, 1),
             False: dot_parts(hot3, gl_s[...], ACROSS, 2, 1)}
     seg_s[...] = jnp.zeros_like(seg_s)
@@ -353,9 +507,7 @@
     for c in range(1, cores):
         push(seg_s.at[(core + c) % cores], segin.at[c], "s0", c, on_core(c))
 
-    for k in range(1, planes):
-        grads.relay_z(k)
-
+    mark("m_t1")
     total = top1[chip]
     for k in range(1, chips):
         arrive(topx.at[k], "t1", k)
@@ -364,6 +516,7 @@
     for k in range(1, planes):
         push(topz.at[plane], topz.at[plane], "t2", k, on_plane(k))
 
+    mark("m_s0")
     total = seg_s[core]
     for c in range(1, cores):
         arrive(segin.at[c], "s0", c)
@@ -372,9 +525,24 @@
     for k in range(1, chips):
         push(seg1.at[(chip + k) % chips], segx.at[k], "s1", k, on_chip(k))
 
+    mark("m_dx")
     for k in range(planes):
-        grads.relay_x(k)
-
+        digits.relay_x(k)
+    mark("m_gz")
+    for k in range(1, planes):
+        grads.relay_z(k)
+    mark("m_df")
+    for k in range(planes):
+        digits.finish(k)
+    mark("m_rank")
+    groups = cores * planes * chips
+    count = rank_lookups(
+        plan, digits_ref[...].reshape(groups, *digits_ref.shape[3:]), rank_s, vals_s)
+    count_ref[...] = jnp.broadcast_to(count, count_ref.shape)
+    mark("m_pick")
+    pick_into(found_s, 0, rank_s, vals_s)
+
+    mark("m_s1")
     total = seg1[chip]
     for k in range(1, chips):
         arrive(segx.at[k], "s1", k)
@@ -392,6 +560,7 @@
             for k in range(1, planes):
                 out_of(p, k).start()
 
+    mark("m_t2")
     for k in range(1, planes):
         arrive(topz.at[back(plane, k, planes)], "t2", k)
     total = topz[0]
@@ -400,6 +569,14 @@
     top_ref[core, chip] = total
     for k in range(1, chips):
         push(top_ref.at[core, chip], top_ref.at[core, chip], "t3", k, on_chip(k))
+
+    mark("m_factors")
+    factors_into(fsel_s, lsel_s, found_s, c1, c3)
+    mark("m_gx")
+    for k in range(planes):
+        grads.relay_x(k)
+
+    mark("m_s2")
 
     def to_owner(p):
         seg = plan.segs[p]
@@ -420,11 +597,25 @@
             def _():
                 to_owner(p).start()
 
+    mark("m_gfin")
+    for k in range(planes):
+        grads.finish(k)
+    saves = [pltpu.make_async_copy(digits_ref, digits_out, save_sems.at[0]),
+             pltpu.make_async_copy(gp_ref, gp_out, save_sems.at[1])]
+    for save in saves:
+        save.start()
+    mark("m_mid")
+    mid_ref[...] = middle_sum(
+        plan, gp_ref[...].reshape(groups * samples, WIDTH), samples,
+        found_s, fsel_s, lsel_s, gsel_s, glsel_s)
+
+    mark("m_t3")
     for k in range(1, chips):
         arrive(top_ref.at[core, back(chip, k, chips)], "t3", k)
     for c in range(1, cores):
         push(top_ref.at[core], top_ref.at[core], "t4", c, on_core(c))
 
+    mark("m_s3")
     for p in range(planes):
         seg = plan.segs[p]
 
@@ -437,11 +628,12 @@
                     if (c, q) != (own_core, own_chip):
                         arrive(seg_ref.at[c, q, :seg.rows], "s3", c * chips + q)
 
-    for k in range(planes):
-        digits.finish(k)
-        grads.finish(k)
+    mark("m_t4")
     for c in range(1, cores):
         arrive(top_ref.at[back(core, c, cores)], "t4", c)
+    mark("m_sent")
+    for save in saves:
+        save.wait()
     for copy in sent:
         copy.wait_send()
     for p in range(planes):
@@ -453,34 +645,43 @@
             @pl.when(gx != plan.segs[p].owner)
             def _():
                 to_owner(p).wait_send()
-
-
-def step_part(plan, *inputs):
+    mark(None)
+
+
+def step_part(plan, chunk, *inputs):
     c1, c2, c3, dense, w, bias, wout, labels, bag, d1, d2, d3 = inputs
     samples, looks = dense.shape[0], d1.shape[1]
     cores, chips, planes = plan.cores, plan.chips, plan.planes
-    shape = lambda *dims: jax.ShapeDtypeStruct(dims, F32)
+    groups = cores * chips * planes
     vmem = pl.BlockSpec(memory_space=pltpu.VMEM)
+    hbm = pl.BlockSpec(memory_space=pltpu.HBM)
     scratch = [R * SIDE, D1 * R, R * D3, R * D3, D1 * SIDE, D1 * SIDE, WIDTH, WIDTH, D1 * R, R * D3]
     top, seg = (plan.trows, LANES), (plan.srows, LANES)
+    digits = (cores, planes, chips, up(4 * looks // LANES, 8), LANES)
+    grads = (cores, planes, chips, samples, WIDTH)
     sums = [
+        digits, grads,
         (cores, chips, *top), (cores, chips, *top), (chips, *top), (chips, *top), (planes, *top),
         (cores, chips, *seg), (cores, chips, *seg), (chips, *seg), (chips, *seg), seg,
         (planes, plan.smost, LANES), (plan.smost, LANES)]
+    inputs = [pltpu.with_memory_space_constraint(x, pltpu.HBM) for x in inputs]
     return pl.pallas_call(
         functools.partial(step_kernel, plan),
-        in_specs=[pl.BlockSpec(memory_space=pltpu.HBM)] * len(inputs),
-        out_specs=(vmem,) * 4,
+        in_specs=[hbm] * len(inputs),
+        out_specs=(hbm, hbm, vmem, vmem, vmem, vmem),
         out_shape=(
-            shape(cores, planes, chips, up(4 * looks // LANES, 8), LANES),
-            shape(cores, planes, chips, samples, WIDTH),
-            shape(cores, chips, *top),
-            shape(cores, chips, plan.smost, LANES),
+            pltpu.HBM(digits, F32),
+            pltpu.HBM(grads, F32),
+            pltpu.VMEM((cores, chips, *top), F32),
+            pltpu.VMEM((cores, chips, plan.smost, LANES), F32),
+            pltpu.VMEM((plan.window * R, SIDE), F32),
+            pltpu.VMEM((8, LANES), F32),
         ),
         scratch_shapes=[pltpu.VMEM(x.shape, x.dtype) for x in inputs]
         + [pltpu.VMEM((rows, looks), F32) for rows in scratch]
         + [pltpu.VMEM(dims, F32) for dims in sums]
-        + [pltpu.SemaphoreType.DMA((len(inputs),))]
+        + select_scratch(groups, looks, chunk)
+        + [pltpu.SemaphoreType.DMA((len(inputs) + 3,)), pltpu.SemaphoreType.DMA((2,))]
         + [pltpu.SemaphoreType.DMA((size,)) for size in stage_sizes(plan) for _ in range(2)],
         compiler_params=pltpu.CompilerParams(
             collective_id=0, has_side_effects=True, vmem_limit_bytes=40 << 20),
@@ -489,80 +690,48 @@
 
 
 def finish_kernel(
-    plan, chunk, c1, c3, digits_in, gp_in, top, seg_in, core_ref, top_ref,
-    rank_s, vals_s, g_s, lastd_s, gleft_s, big_s,
+    plan, c1_in, c3_in, digits_in, gp_in, top, seg_in, mid, count_in, core_out, top_out,
+    c1, c3, blocks_s, gp_s, rank_s, vals_s, found_s, fsel_s, lsel_s, gsel_s, glsel_s,
+    big_s, core_s, top_s, more_sems, out_sems,
 ):
     cores, chips, planes, window = plan.cores, plan.chips, plan.planes, plan.window
     gx, plane = lax.axis_index("gx"), lax.axis_index("gy")
-    start = (gx * planes + plane) * plan.share
-    r0 = jnp.clip((start - plan.n1) // plan.row, 0, plan.n2_rows - window)
-    samples = gp_in.shape[3]
-    groups = cores * planes * chips
-    gp = gp_in[...].reshape(groups * samples, WIDTH)
-    blocks = digits_in[...].reshape(groups, *digits_in.shape[3:])
+    r0, start = first_row(plan)
+    chunk = found_s.shape[1]
 
     deep = plan.trows - 8
     for h in range(cores):
         lanes = slice(h * LANES, (h + 1) * LANES)
         for q in range(chips):
-            top_ref[q * deep:(q + 1) * deep, lanes] = top[h, q, :deep, :]
-        top_ref[chips * deep:, lanes] = top[h, 0, deep:deep + 2, :]
-
-    looks = rank_s.shape[1]
-    per = looks // LANES
-    digits = [
-        jnp.concatenate([blocks[:, k * per + h, :] for h in range(per)], axis=1).astype(jnp.int32)
-        for k in range(4)
-    ]
-    rel = digits[2] - r0
-    inside = (rel >= 0) & (rel < window)
-    low = jnp.where(inside, 1.0, 0.0).astype(BF16)
-    tri = jnp.where(
-        lax.broadcasted_iota(jnp.int32, (looks, looks), 0)
-        < lax.broadcasted_iota(jnp.int32, (looks, looks), 1), 1.0, 0.0).astype(BF16)
-    above = jnp.where(
-        lax.broadcasted_iota(jnp.int32, (groups, groups), 0)
-        > lax.broadcasted_iota(jnp.int32, (groups, groups), 1), 1.0, 0.0).astype(BF16)
-    before = jnp.sum(dot(above, low, PLAIN), axis=1, keepdims=True)
-    rank_s[...] = jnp.where(inside, dot(low, tri, PLAIN) + before, -1.0).astype(jnp.int32)
-    count = jnp.sum(jnp.where(inside, 1, 0))
-    group = lax.broadcasted_iota(jnp.int32, (groups, looks), 0)
-    columns = (digits[0], digits[1], digits[3], group, jnp.where(inside, rel + 1, 0))
-    for k, column in enumerate(columns):
-        vals_s[:, k:k + 1, :] = column.astype(F32).reshape(groups, 1, looks)
-    vals_s[:, len(columns):, :] = jnp.zeros((groups, 8 - len(columns), looks), F32)
-    base = plan.n1 // LANES
-    rows = window * R
-    big_s[base:base + rows, :] = jnp.zeros((rows, LANES), F32)
-    gp_high, gp_low = parts_of(gp, 2)
-    slots = lax.broadcasted_iota(jnp.int32, (chunk, looks), 0)
-
-    def body(step, carry):
-        def pick(e, found):
-            ranks = rank_s[pl.ds(e, 1), :] - step * chunk
-            chosen = jnp.where(slots == ranks, 1.0, 0.0).astype(BF16)
-            return found + dot(vals_s[e].astype(BF16), chosen, ACROSS)
-
-        found = lax.fori_loop(0, groups, pick, jnp.zeros((8, chunk), F32), unroll=4)
-        found = found.astype(jnp.int32)
-        bag, d1, d3, owner, rel1 = (found[k:k + 1, :] for k in range(5))
-        first = dot(c1[...], hot(d1, c1.shape[0], BF16), DOWN)
-        last = dot(c3[...], hot(d3, c3.shape[0], BF16), DOWN)
-        lastd_s[...] = by_d3(last.astype(BF16))
-        sample = hot(owner * samples + bag, gp.shape[0], BF16)
-        g_s[...] = dot(gp_high, sample, DOWN) + dot(gp_low, sample, DOWN)
-        grad_left_into(gleft_s, g_s, lastd_s)
-        total = big_s[base:base + rows, :]
-        for i in range(D1):
-            part = first[i * R:(i + 1) * R, :]
-            spread = jnp.concatenate(
-                [jnp.where(rel1 == r + 1, part, 0.0) for r in range(window)], axis=0
-            ).astype(BF16)
-            total = total + dot_parts(spread, gleft_s[i * SIDE:(i + 1) * SIDE, :], ACROSS, 2, 1)
-        big_s[base:base + rows, :] = total
-        return carry
-
-    lax.fori_loop(0, (count + chunk - 1) // chunk, body, 0)
+            top_s[q * deep:(q + 1) * deep, lanes] = top[h, q, :deep, :]
+        top_s[chips * deep:, lanes] = top[h, 0, deep:deep + 2, :]
+    save_top = pltpu.make_async_copy(top_s, top_out, out_sems.at[0])
+    save_top.start()
+
+    base, rows = plan.n1 // LANES, window * R
+    big_s[base:base + rows, :] = mid[...]
+    count = jnp.max(count_in[...]).astype(jnp.int32)
+
+    @pl.when(count > chunk)
+    def _():
+        pairs = zip((c1_in, c3_in, digits_in, gp_in), (c1, c3, blocks_s, gp_s))
+        loads = [pltpu.make_async_copy(a, b, more_sems.at[k]) for k, (a, b) in enumerate(pairs)]
+        for load in loads:
+            load.start()
+        for load in loads:
+            load.wait()
+        groups, samples = rank_s.shape[0], gp_s.shape[3]
+        rank_lookups(plan, blocks_s[...].reshape(groups, *blocks_s.shape[3:]), rank_s, vals_s)
+
+        def body(step, carry):
+            pick_into(found_s, step, rank_s, vals_s)
+            factors_into(fsel_s, lsel_s, found_s, c1, c3)
+            big_s[base:base + rows, :] = big_s[base:base + rows, :] + middle_sum(
+                plan, gp_s[...].reshape(groups * samples, WIDTH), samples,
+                found_s, fsel_s, lsel_s, gsel_s, glsel_s)
+            return carry
+
+        lax.fori_loop(1, (count + chunk - 1) // chunk, body, 0)
 
     halves = seg_in.shape[0]
     for p in range(planes):
@@ -579,46 +748,48 @@
 
     at = start // LANES - r0 * (plan.row // LANES)
     shift = start % LANES
-    count = core_ref.shape[0]
-    here, after = big_s[pl.ds(at, count), :], big_s[pl.ds(at + 1, count), :]
+    size = core_s.shape[0]
+    here, after = big_s[pl.ds(at, size), :], big_s[pl.ds(at + 1, size), :]
     turn = (LANES - shift) % LANES
-    lane = lax.broadcasted_iota(jnp.int32, (count, LANES), 1)
-    core_ref[...] = jnp.where(
+    lane = lax.broadcasted_iota(jnp.int32, (size, LANES), 1)
+    core_s[...] = jnp.where(
         lane < LANES - shift, pltpu.roll(here, turn, 1), pltpu.roll(after, turn, 1))
-
-
-def finish_part(plan, looks, c1, c3, digits, gp, top, seg):
+    save_core = pltpu.make_async_copy(core_s, core_out, out_sems.at[1])
+    save_core.start()
+    save_top.wait()
+    save_core.wait()
+
+
+def finish_part(plan, chunk, looks, c1, c3, digits, gp, top, seg, mid, count):
     groups = plan.cores * plan.chips * plan.planes
-    chunk = 512
     vmem = pl.BlockSpec(memory_space=pltpu.VMEM)
-    last_rows = plan.n3_rows * seg.shape[0]
+    hbm = pl.BlockSpec(memory_space=pltpu.HBM)
     out_rows = up(-(-plan.share // LANES), 8)
-    big = up(plan.n1 // LANES + plan.window * R + last_rows + out_rows, 8)
+    big = up(plan.n1 // LANES + plan.window * R + plan.n3_rows * seg.shape[0] + out_rows, 8)
+    core_shape = (out_rows, LANES)
+    top_shape = (plan.chips * (plan.trows - 8) + 2, plan.cores * LANES)
+    far = [pltpu.with_memory_space_constraint(x, pltpu.HBM) for x in (c1, c3, digits, gp)]
     return pl.pallas_call(
-        functools.partial(finish_kernel, plan, chunk),
-        out_shape=(
-            jax.ShapeDtypeStruct((out_rows, LANES), F32),
-            jax.ShapeDtypeStruct((plan.chips * (plan.trows - 8) + 2, plan.cores * LANES), F32),
-        ),
-        in_specs=[vmem] * 6,
-        out_specs=(vmem, vmem),
-        scratch_shapes=[
-            pltpu.VMEM((groups, looks), jnp.int32),
-            pltpu.VMEM((groups, 8, looks), F32),
-            pltpu.VMEM((WIDTH, chunk), F32),
-            pltpu.VMEM((R * D3, chunk), F32),
-            pltpu.VMEM((D1 * SIDE, chunk), F32),
-            pltpu.VMEM((big, LANES), F32),
-        ],
+        functools.partial(finish_kernel, plan),
+        out_shape=(pltpu.HBM(core_shape, F32), pltpu.HBM(top_shape, F32)),
+        in_specs=[hbm] * 4 + [vmem] * 4,
+        out_specs=(hbm, hbm),
+        scratch_shapes=[pltpu.VMEM(x.shape, x.dtype) for x in (c1, c3, digits, gp)]
+        + select_scratch(groups, looks, chunk)
+        + [pltpu.VMEM((big, LANES), F32), pltpu.VMEM(core_shape, F32),
+           pltpu.VMEM(top_shape, F32), pltpu.SemaphoreType.DMA((4,)), pltpu.SemaphoreType.DMA((2,))],
         compiler_params=pltpu.CompilerParams(vmem_limit_bytes=40 << 20),
         name="finish",
-    )(c1, c3, digits, gp, top, seg)
+    )(*far, top, seg, mid, count)
 
 
 def per_device(plan, c1, c2, c3, dense, w, bias, wout, labels, bag, d1, d2, d3):
-    digits, gp, top, seg = step_part(
-        plan, c1, c2, c3, dense, w, bias[None], wout[None], labels[None], bag, d1, d2, d3)
-    core, top = finish_part(plan, d1.shape[1], c1, c3, digits, gp, top, seg)
+    looks = d1.shape[1]
+    expected = plan.nx * plan.ny * looks * plan.window // plan.n2_rows
+    chunk = up(expected * 9 // 8, LANES)
+    digits, gp, top, seg, mid, count = step_part(
+        plan, chunk, c1, c2, c3, dense, w, bias[None], wout[None], labels[None], bag, d1, d2, d3)
+    core, top = finish_part(plan, chunk, looks, c1, c3, digits, gp, top, seg, mid, count)
     return core.reshape(-1)[:plan.share], top
 
 

time: 50.4 us -> 33.1 us (0.66)
  local copies, waits for them, and re-layouts: 9.48 us -> 0 us
  Pallas kernels: 39.8 us -> 32.3 us
    unnamed x26 -> x0, local copies, waits for them, and re-layouts: 9.48 us -> none
    pallas_call x2, Pallas kernels: 39.8 us -> 32.3 us  [the longest x1 31.3 us: step_part(): pl.pallas_call(functools.partial(step_kernel, plan), in_specs=[hbm] * len...]
where the time goes in v1:
time: 33.1 us; the launch traced here: 32.9 us
  Pallas kernels  32.3 us (98%)
  between operations  0.64 us (2%)
    pallas_call x1, Pallas kernels, step_part(): pl.pallas_call(functools.partial(step_kernel, plan), in_specs=[hbm] * len...  31.3 us
    pallas_call x1, Pallas kernels, finish_part(): pl.pallas_call(functools.partial(finish_kernel, plan), out_shape=(pltpu.H...  0.98 us

profile of v1, /device:TPU:0, one launch (start us, length us, event | category | flops | bytes accessed | tf_op | source)
XLA Modules:
  0.0 32.9 jit_solution(5214737614895471919)
XLA Ops:
  0.6 31.3 %step.1 = (f32[2,4,4,8,128]{4,3,2,1,0:T(8,128)}, f32[2,4,4,64,128]{4,3,2,1,0:T(8,128)}, f32[2,4,72,128]{3,2,1,0:T(8,128)S(1)}, f32[2,4,32,128]{3,2,1,0:T(8,128)S...) custom-call(bf16[200,128]{1,0:T(8,128)(2,1)} %c1_in.1, bf16[200,4096]{1,0:T(8,128)(2,1)} %refs_1_.1, ...), custom_call_target="tpu_custom_call" | custom-call | tf_op jit(solution)/shard_map/step/pallas_call | solution.py:668
  32.0 1.0 %finish.1 = (f32[224,128]{1,0:T(8,128)}, f32[258,256]{1,0:T(8,128)}) custom-call(bf16[200,128]{1,0:T(8,128)(2,1)} %c1_in.1, bf16[250,256]{1,0:T(8,128)(2,1)} %c3_in.1, f32[2,4,4,8,128]{4,3,2,1,0:T(8,128)} %get-tuple-element.10.digits_in, f32[2,4,4,64,128]{4,3,2,1,0:T(8,128)} %get-tuple-element.11.gp_in, f32[2,4,72,128]{3,2,1,0:T(8,128)S(1)} %get-tuple-element.12.top, ...), custom_call_target="tpu_custom_call" | custom-call | tf_op jit(solution)/shard_map/finish/pallas_call | solution.py:772

commit v2 on v1

--- a/solution.py
+++ b/solution.py
@@ -16,6 +16,7 @@
 PAIRS = D1 * D2
 SIDE = D2 * R
 LANES = 128
+LOCAL = 32
 AXES = ("gx", "gy")
 F32 = jnp.float32
 BF16 = jnp.bfloat16
@@ -39,10 +40,14 @@
 
 
 def dot_parts(a, b, dims, count, wide):
+    free = 1 - dims[wide][0]
+    joined = jnp.concatenate(parts_of((a, b)[wide], count), axis=free)
+    out = dot(joined, b, dims) if wide == 0 else dot(a, joined, dims)
+    size = out.shape[wide] // count
     total = None
-    for part in parts_of((a, b)[wide], count):
-        term = dot(part, b, dims) if wide == 0 else dot(a, part, dims)
-        total = term if total is None else total + term
+    for k in range(count):
+        part = lax.slice_in_dim(out, k * size, (k + 1) * size, axis=wide)
+        total = part if total is None else total + part
     return total
 
 
@@ -148,10 +153,12 @@
     @pl.loop(0, PAIRS // batch)
     def _(b):
         totals = [None] * batch
+        left = left_s.at[pl.ds(pl.multiple_of(b * batch * R, batch * R), batch * R), :]
         for c in range(R):
             last = last_s[c * D3:(c + 1) * D3, :]
             for k in range(batch):
-                totals[k] = add(totals[k], left_s[pl.ds((b * batch + k) * R + c, 1), :] * last)
+                row = k * R + c
+                totals[k] = add(totals[k], left[row:row + 1, :] * last)
         for k in range(batch):
             emb_s[pl.ds(pl.multiple_of((b * batch + k) * D3, D3), D3), :] = totals[k]
 
@@ -162,10 +169,12 @@
     @pl.loop(0, PAIRS // batch)
     def _(b):
         totals = [None] * batch
+        g = g_s.at[pl.ds(pl.multiple_of(b * batch * D3, batch * D3), batch * D3), :]
         for d in range(D3):
             last = lastd_s[d * R:(d + 1) * R, :]
             for k in range(batch):
-                totals[k] = add(totals[k], g_s[pl.ds((b * batch + k) * D3 + d, 1), :] * last)
+                row = k * D3 + d
+                totals[k] = add(totals[k], g[row:row + 1, :] * last)
         for k in range(batch):
             gleft_s[pl.ds(pl.multiple_of((b * batch + k) * R, R), R), :] = totals[k]
 
@@ -174,10 +183,12 @@
     @pl.loop(0, R // batch)
     def _(b):
         totals = [None] * batch
+        left = left_s.at[pl.ds(pl.multiple_of(b * batch, batch), (PAIRS - 1) * R + batch), :]
         for p in range(PAIRS):
             g = g_s[p * D3:(p + 1) * D3, :]
             for k in range(batch):
-                totals[k] = add(totals[k], left_s[pl.ds(p * R + b * batch + k, 1), :] * g)
+                row = p * R + k
+                totals[k] = add(totals[k], left[row:row + 1, :] * g)
         for k in range(batch):
             gl_s[pl.ds(pl.multiple_of((b * batch + k) * D3, D3), D3), :] = totals[k]
 
@@ -185,13 +196,15 @@
 def grad_first_into(gf_s, gleft_s, mid_s, batch=8):
     def body(b, lanes):
         totals = [[None] * D1 for _ in range(batch)]
+        size = batch * SIDE
+        mid = mid_s.at[pl.ds(pl.multiple_of(b * size, size), size), lanes]
+        gleft = gleft_s.at[:, lanes]
         for t in range(0, SIDE, 8):
-            gleft = [gleft_s[i * SIDE + t:i * SIDE + t + 8, lanes] for i in range(D1)]
+            rows = [gleft[i * SIDE + t:i * SIDE + t + 8, :] for i in range(D1)]
             for k in range(batch):
-                at = pl.multiple_of((b * batch + k) * SIDE + t, 8)
-                m = mid_s[pl.ds(at, 8), lanes]
+                m = mid[k * SIDE + t:k * SIDE + t + 8, :]
                 for i in range(D1):
-                    totals[k][i] = add(totals[k][i], gleft[i] * m)
+                    totals[k][i] = add(totals[k][i], rows[i] * m)
         for i in range(D1):
             rows = [jnp.sum(totals[k][i], axis=0, keepdims=True) for k in range(batch)]
             gf_s[pl.ds(pl.multiple_of(i * R + b * batch, 8), batch), lanes] = (
@@ -205,7 +218,7 @@
     return jnp.clip((start - plan.n1) // plan.row, 0, plan.n2_rows - plan.window), start
 
 
-def rank_lookups(plan, blocks, rank_s, vals_s):
+def rank_lookups(plan, blocks, rank_s, vals_s, local_s=None):
     groups, looks = rank_s.shape
     per = looks // LANES
     r0, _ = first_row(plan)
@@ -223,13 +236,19 @@
         lax.broadcasted_iota(jnp.int32, (groups, groups), 0)
         > lax.broadcasted_iota(jnp.int32, (groups, groups), 1), 1.0, 0.0).astype(BF16)
     before = jnp.sum(dot(above, low, PLAIN), axis=1, keepdims=True)
-    rank_s[...] = jnp.where(inside, dot(low, tri, PLAIN) + before, -1.0).astype(jnp.int32)
+    local = dot(low, tri, PLAIN)
+    rank = jnp.where(inside, local + before, -1.0).astype(jnp.int32)
+    rank_s[...] = rank
+    if local_s is not None:
+        local_s[...] = jnp.where(inside, local, -1.0).astype(jnp.int32)
     group = lax.broadcasted_iota(jnp.int32, (groups, looks), 0)
-    columns = (digits[0], digits[1], digits[3], group, jnp.where(inside, rel + 1, 0))
+    columns = (digits[0], digits[1], digits[3], group, jnp.where(inside, rel + 1, 0),
+               (rank + 1) // LANES, (rank + 1) % LANES)
     for k, column in enumerate(columns):
         vals_s[:, k:k + 1, :] = column.astype(F32).reshape(groups, 1, looks)
     vals_s[:, len(columns):, :] = jnp.zeros((groups, 8 - len(columns), looks), F32)
-    return jnp.sum(jnp.where(inside, 1.0, 0.0), axis=(0, 1), keepdims=True)
+    each = jnp.sum(jnp.where(inside, 1.0, 0.0), axis=1, keepdims=True)
+    return jnp.sum(each, axis=0, keepdims=True), jnp.max(each, axis=0, keepdims=True)
 
 
 def pick_into(found_s, step, rank_s, vals_s):
@@ -246,61 +265,70 @@
     found_s[...] = found.astype(jnp.int32)
 
 
-def factors_into(fsel_s, lsel_s, found_s, c1, c3):
-    fsel_s[...] = dot(c1[...], hot(found_s[1:2, :], c1.shape[0], BF16), DOWN)
+def pick_few_into(found_s, local_s, vals_s, few_s):
+    groups, looks = local_s.shape
+    cap = few_s.shape[0] // groups
+    slots = lax.broadcasted_iota(jnp.int32, (cap, looks), 0)
+    for e in range(groups):
+        chosen = jnp.where(slots == local_s[e:e + 1, :], 1.0, 0.0).astype(BF16)
+        few_s[e * cap:(e + 1) * cap, :] = dot(chosen, vals_s[e].astype(BF16), ACROSS)
+    few = few_s[...]
+    ranks = (few[:, 5:6] * LANES + few[:, 6:7]).astype(jnp.int32) - 1
+    slots = lax.broadcasted_iota(jnp.int32, (few.shape[0], found_s.shape[1]), 1)
+    chosen = jnp.where(slots == ranks, 1.0, 0.0).astype(BF16)
+    found_s[...] = dot(few.astype(BF16), chosen, DOWN).astype(jnp.int32)
+
+
+def factors_into(plan, samples, spread_s, lsel_s, sample_s, found_s, c1, c3):
+    first = dot(c1[...], hot(found_s[1:2, :], c1.shape[0], BF16), DOWN)
     last = dot(c3[...], hot(found_s[2:3, :], c3.shape[0], BF16), DOWN)
     lsel_s[...] = by_d3(last.astype(BF16))
-
-
-def middle_sum(plan, gp, samples, found_s, fsel_s, lsel_s, gsel_s, glsel_s):
-    sample = hot(found_s[3:4, :] * samples + found_s[0:1, :], gp.shape[0], BF16)
-    gsel_s[...] = dot_parts(gp, sample, DOWN, 2, 0)
+    rel1 = found_s[4:5, :]
+    for i in range(D1):
+        part = first[i * R:(i + 1) * R, :]
+        for r in range(plan.window):
+            row = (i * plan.window + r) * R
+            spread_s[row:row + R, :] = jnp.where(rel1 == r + 1, part, 0.0).astype(BF16)
+    sample_s[...] = hot(found_s[3:4, :] * samples + found_s[0:1, :], sample_s.shape[0], BF16)
+
+
+def middle_sum(plan, spread_s, lsel_s, gsel_s, glsel_s):
     grad_left_into(glsel_s, gsel_s, lsel_s)
-    rel1 = found_s[4:5, :]
+    rows = plan.window * R
     total = None
     for i in range(D1):
-        part = fsel_s[i * R:(i + 1) * R, :]
-        spread = jnp.concatenate(
-            [jnp.where(rel1 == r + 1, part, 0.0) for r in range(plan.window)], axis=0
-        ).astype(BF16)
-        total = add(total, dot_parts(spread, glsel_s[i * SIDE:(i + 1) * SIDE, :], ACROSS, 2, 1))
+        total = add(total, dot_parts(
+            spread_s[i * rows:(i + 1) * rows, :], glsel_s[i * SIDE:(i + 1) * SIDE, :],
+            ACROSS, 2, 1))
     return total
 
 
-def select_scratch(groups, looks, chunk):
+def select_scratch(plan, looks, samples, chunk):
+    groups = plan.cores * plan.chips * plan.planes
     return [
         pltpu.VMEM((groups, looks), jnp.int32),
         pltpu.VMEM((groups, 8, looks), F32),
         pltpu.VMEM((8, chunk), jnp.int32),
-        pltpu.VMEM((D1 * R, chunk), F32),
+        pltpu.VMEM((D1 * plan.window * R, chunk), BF16),
         pltpu.VMEM((R * D3, chunk), F32),
+        pltpu.VMEM((groups * samples, chunk), BF16),
         pltpu.VMEM((WIDTH, chunk), F32),
         pltpu.VMEM((D1 * SIDE, chunk), F32),
     ]
 
 
-STAGES = ("dz", "dx", "dc", "gz", "gx", "gc", "t0", "t1", "t2", "t3", "t4", "s0", "s1", "s2", "s3")
-
-
-def stage_sizes(plan):
-    cores, chips, planes = plan.cores, plan.chips, plan.planes
-    gather = dict(z=planes, x=chips * planes, c=cores * planes)
-    sizes = {kind + axis: size for kind in "dg" for axis, size in gather.items()}
-    sizes.update(t0=cores, t1=chips, t2=planes, t3=chips, t4=cores,
-                 s0=cores, s1=chips, s2=planes, s3=cores * chips)
-    return [sizes[name] for name in STAGES]
+STAGES = ("dz", "dx", "dc", "gz", "gx", "gc", "bx", "bz", "t0", "t1", "t2", "t3", "t4", "s0", "s1", "s2", "s3")
 
 
 def step_kernel(plan, *refs):
     inputs, refs = refs[:12], refs[12:]
-    digits_out, gp_out, top_ref, seg_ref, mid_ref, count_ref = refs[:6]
+    digits_out, gp_out, top_ref, seg_ref, mid_ref, rest_ref = refs[:6]
     held, refs = refs[6:18], refs[18:]
     mid_s, first_s, last_s, lastd_s, left_s, gleft_s, emb_s, g_s, gf_s, gl_s = refs[:10]
     digits_ref, gp_ref = refs[10:12]
-    top_s, topin, top1, topx, topz, seg_s, segin, seg1, segx, seg2, segz, seg3 = refs[12:24]
-    rank_s, vals_s, found_s, fsel_s, lsel_s, gsel_s, glsel_s = refs[24:31]
-    load_sems, save_sems, sems = refs[31], refs[32], refs[33:]
-    sems = {name: (sems[2 * i], sems[2 * i + 1]) for i, name in enumerate(STAGES)}
+    top_s, topin, top1, topx, topz, seg_s, segin, seg1, segx, seg2, segz, seg3, segall = refs[12:25]
+    rank_s, vals_s, found_s, spread_s, lsel_s, sample_s, gsel_s, glsel_s = refs[25:33]
+    local_s, few_s, load_sems, save_sems, send_sems, recv_sems, grad_sems = refs[33:40]
     cores, chips, planes = plan.cores, plan.chips, plan.planes
     gx, plane = lax.axis_index("gx"), lax.axis_index("gy")
     core, chip = gx % cores, gx // cores
@@ -315,7 +343,7 @@
 
     mark("m_start")
     c1, c2, c3, dense, w, bias, wout, labels, bag, d1, d2, d3 = held
-    wide = c2.shape[1] // 4
+    wide = c2.shape[1] // 2
     loads = {}
 
     def load(k, columns=None):
@@ -328,9 +356,9 @@
         return n
 
     early = [load(k) for k in (10, 9, 11, 8)]
+    early += [load(k) for k in (0, 2)]
     tables = [load(1, slice(lo, lo + wide)) for lo in range(0, c2.shape[1], wide)]
-    early += [load(0)]
-    late = [load(k) for k in (2, 3, 4, 5, 6, 7)]
+    late = [load(k) for k in (3, 4, 5, 6, 7)]
 
     def at(c, q, p):
         return (q * cores + c, p)
@@ -351,59 +379,40 @@
     for peer in peers:
         pl.semaphore_signal(barrier, inc=1, device_id=peer, device_id_type=pl.DeviceIdType.MESH)
 
-    sent = []
-
-    def remote(src, dst, stage, k, peer):
+    def remote(src, dst, stage, peer, grad=None):
+        n = STAGES.index(stage)
         return pltpu.make_async_remote_copy(
-            src_ref=src, dst_ref=dst, send_sem=sems[stage][0].at[k],
-            recv_sem=sems[stage][1].at[k], device_id=peer,
+            src_ref=src, dst_ref=dst, send_sem=send_sems.at[n],
+            recv_sem=recv_sems.at[n] if grad is None else grad_sems.at[grad], device_id=peer,
             device_id_type=pl.DeviceIdType.MESH)
 
-    def push(src, dst, stage, k, peer):
-        copy = remote(src, dst, stage, k, peer)
-        copy.start()
-        sent.append(copy)
-
-    def arrive(ref, stage, k):
-        remote(ref, ref, stage, k, on_plane(1)).wait_recv()
+    def push(src, dst, stage, peer, grad=None):
+        remote(src, dst, stage, peer, grad).start()
+
+    def arrive(like, stage, grad=None):
+        remote(like, like, stage, on_core(1), grad).wait_recv()
+
+    def leave(like, stage):
+        remote(like, like, stage, on_core(1)).wait_send()
 
     def back(me, k, size):
         return (me + size - k) % size
 
-    class Gather:
-        def __init__(self, ref, kind):
-            self.ref, self.kind = ref, kind
-
-        def own_z(self):
-            slot = self.ref.at[core, plane, chip]
-            for k in range(1, planes):
-                push(slot, slot, self.kind + "z", k, on_plane(k))
-
-        def own_x(self):
-            slot = self.ref.at[core, plane, chip]
-            for q in range(1, chips):
-                push(slot, slot, self.kind + "x", q * planes, on_chip(q))
-
-        def relay_z(self, k):
-            slot = self.ref.at[core, back(plane, k, planes), chip]
-            arrive(slot, self.kind + "z", k)
-            for q in range(1, chips):
-                push(slot, slot, self.kind + "x", q * planes + k, on_chip(q))
-
-        def relay_x(self, k):
-            z = back(plane, k, planes)
-            for q in range(1, chips):
-                arrive(self.ref.at[core, z, back(chip, q, chips)], self.kind + "x", q * planes + k)
-            slot = self.ref.at[core, z]
-            for c in range(1, cores):
-                push(slot, slot, self.kind + "c", c * planes + k, on_core(c))
-
-        def finish(self, k):
-            for c in range(1, cores):
-                slot = self.ref.at[back(core, c, cores), back(plane, k, planes)]
-                arrive(slot, self.kind + "c", c * planes + k)
-
-    digits, grads = Gather(digits_ref, "d"), Gather(gp_ref, "g")
+    def own_z(ref, kind, rows=slice(None)):
+        slot = ref.at[core, plane, chip, rows]
+        for k in range(1, planes):
+            push(slot, slot, kind + "z", on_plane(k))
+
+    def push_x(ref, kind, k, grad=None, rows=slice(None)):
+        slot = ref.at[core, back(plane, k, planes), chip, rows]
+        for q in range(1, chips):
+            push(slot, slot, kind + "x", on_chip(q), grad)
+
+    def of_z(ref, rows=slice(None)):
+        return ref.at[0, :planes - 1, 0, rows]
+
+    def of_x(ref, rows=slice(None)):
+        return ref.at[0, :, :chips - 1, rows]
 
     mark("m_gather")
     for n in early:
@@ -416,24 +425,24 @@
                 digit[:, h * LANES:(h + 1) * LANES].astype(F32))
     hot1 = hot(d1[...], c1.shape[0], BF16)
     hot2 = hot(d2[...], c2.shape[0], BF16)
+    hot3 = hot(d3[...], c3.shape[0], BF16)
     first_s[...] = dot(c1[...], hot1, DOWN)
+    last_t = dot(c3[...], hot3, DOWN)
+    last_s[...] = last_t
+    lastd_s[...] = by_d3(last_t.astype(BF16))
     for k, n in enumerate(tables):
         loads[n].wait()
         for lo, size in spans(wide, 512):
             lo += k * wide
             mid_s[lo:lo + size, :] = dot(c2[:, lo:lo + size], hot2, DOWN)
+    mark("m_barrier")
+    pl.semaphore_wait(barrier, len(peers))
+    own_z(digits_ref, "d")
+    push_x(digits_ref, "d", 0)
     mark("m_left")
     left_into(left_s, first_s, mid_s)
     for n in late:
         loads[n].wait()
-    hot3 = hot(d3[...], c3.shape[0], BF16)
-    last_t = dot(c3[...], hot3, DOWN)
-    last_s[...] = last_t
-    lastd_s[...] = by_d3(last_t.astype(BF16))
-    mark("m_barrier")
-    pl.semaphore_wait(barrier, len(peers))
-    digits.own_z()
-    digits.own_x()
     mark("m_emb")
     embedded_into(emb_s, left_s, last_s)
 
@@ -469,31 +478,31 @@
             half = weight[lo // WIDTH]
             top_s[h, q, :deep, :] = half[lo % WIDTH:lo % WIDTH + deep, lanes]
             top_s[h, q, deep:, :] = vectors[:, lanes] if q == 0 else jnp.zeros((8, LANES), F32)
-    for c in range(1, cores):
-        push(top_s.at[(core + c) % cores], topin.at[c], "t0", c, on_core(c))
+    push(top_s.at[1 - core], topin, "t0", on_core(1))
     gp = dot(low, w[WIDTH:, :], ACROSS)
     gp_ref[core, plane, chip] = gp
-    grads.own_z()
+    split = samples - samples // 4
+    most, others = slice(0, split), slice(split, samples)
+    push_x(gp_ref, "b", 0, None, others)
+    own_z(gp_ref, "g", most)
 
     mark("m_gleft")
     g_s[...] = dot_parts(gp, bags, DOWN, 2, 0)
-    grad_left_into(gleft_s, g_s, lastd_s)
-
-    mark("m_t0")
-    total = top_s[core]
-    for c in range(1, cores):
-        arrive(topin.at[c], "t0", c)
-        total = total + topin[c]
-    top1[...] = total
-    for k in range(1, chips):
-        push(top1.at[(chip + k) % chips], topx.at[k], "t1", k, on_chip(k))
-    grads.own_x()
-
     mark("m_gl")
     grad_last_into(gl_s, left_s, g_s)
+    mark("m_gleft2")
+    grad_left_into(gleft_s, g_s, lastd_s)
+    mark("m_t0")
+    arrive(topin, "t0")
+    top1[...] = top_s[core] + topin[...]
+    for k in range(1, chips):
+        push(top1.at[(chip + k) % chips], topx.at[k], "t1", on_chip(k))
     mark("m_dz")
+    arrive(of_z(digits_ref), "dz")
     for k in range(1, planes):
-        digits.relay_z(k)
+        push_x(digits_ref, "d", k)
+    push_x(gp_ref, "g", 0, 0, most)
+
     mark("m_gf")
     grad_first_into(gf_s, gleft_s, mid_s)
     mark("m_segdot")
@@ -504,55 +513,57 @@
         for c, q, lo, hi, h in pieces_of(seg, cores, chips, cores):
             seg_s[c, q, seg.offset:seg.offset + hi - lo, :] = (
                 sums[seg.first][lo:hi, h * LANES:(h + 1) * LANES])
-    for c in range(1, cores):
-        push(seg_s.at[(core + c) % cores], segin.at[c], "s0", c, on_core(c))
-
+    push(seg_s.at[1 - core], segin, "s0", on_core(1))
+
+    mark("m_bx")
+    arrive(gp_ref.at[0, 0, :chips - 1, others], "bx")
+    slot = gp_ref.at[core, plane, :, others]
+    for k in range(1, planes):
+        push(slot, slot, "bz", on_plane(k))
+    mark("m_s0")
+    arrive(segin, "s0")
+    seg1[...] = seg_s[core] + segin[...]
+    for k in range(1, chips):
+        push(seg1.at[(chip + k) % chips], segx.at[k], "s1", on_chip(k))
+
+    mark("m_gz")
+    arrive(of_z(gp_ref, most), "gz")
+    for k in range(1, planes):
+        push_x(gp_ref, "g", k, k, most)
     mark("m_t1")
+    arrive(topx.at[1:], "t1")
     total = top1[chip]
     for k in range(1, chips):
-        arrive(topx.at[k], "t1", k)
         total = total + topx[k]
     topz[plane] = total
     for k in range(1, planes):
-        push(topz.at[plane], topz.at[plane], "t2", k, on_plane(k))
-
-    mark("m_s0")
-    total = seg_s[core]
-    for c in range(1, cores):
-        arrive(segin.at[c], "s0", c)
-        total = total + segin[c]
-    seg1[...] = total
-    for k in range(1, chips):
-        push(seg1.at[(chip + k) % chips], segx.at[k], "s1", k, on_chip(k))
+        push(topz.at[plane], topz.at[plane], "t2", on_plane(k))
 
     mark("m_dx")
-    for k in range(planes):
-        digits.relay_x(k)
-    mark("m_gz")
-    for k in range(1, planes):
-        grads.relay_z(k)
+    arrive(of_x(digits_ref), "dx")
+    push(digits_ref.at[core], digits_ref.at[core], "dc", on_core(1))
     mark("m_df")
-    for k in range(planes):
-        digits.finish(k)
+    arrive(digits_ref.at[1 - core], "dc")
     mark("m_rank")
     groups = cores * planes * chips
-    count = rank_lookups(
-        plan, digits_ref[...].reshape(groups, *digits_ref.shape[3:]), rank_s, vals_s)
-    count_ref[...] = jnp.broadcast_to(count, count_ref.shape)
+    count, fullest = rank_lookups(
+        plan, digits_ref[...].reshape(groups, *digits_ref.shape[3:]), rank_s, vals_s, local_s)
+    fits = (count <= found_s.shape[1]) & (fullest <= few_s.shape[0] // groups)
+    rest_ref[...] = jnp.broadcast_to(jnp.where(fits, 0.0, 1.0), rest_ref.shape)
     mark("m_pick")
-    pick_into(found_s, 0, rank_s, vals_s)
+    pick_few_into(found_s, local_s, vals_s, few_s)
 
     mark("m_s1")
+    arrive(segx.at[1:], "s1")
     total = seg1[chip]
     for k in range(1, chips):
-        arrive(segx.at[k], "s1", k)
         total = total + segx[k]
     seg2[...] = total
 
     def out_of(p, k):
         seg = plan.segs[(p + k) % planes]
         return remote(seg2.at[seg.offset:seg.offset + seg.rows],
-                      segz.at[k, :seg.rows], "s2", k, on_plane(k))
+                      segz.at[k, :seg.rows], "s2", on_plane(k))
 
     for p in range(planes):
         @pl.when(plane == p)
@@ -560,36 +571,49 @@
             for k in range(1, planes):
                 out_of(p, k).start()
 
+    mark("m_factors")
+    factors_into(plan, samples, spread_s, lsel_s, sample_s, found_s, c1, c3)
     mark("m_t2")
-    for k in range(1, planes):
-        arrive(topz.at[back(plane, k, planes)], "t2", k)
+    arrive(topz.at[1:], "t2")
     total = topz[0]
     for k in range(1, planes):
         total = total + topz[k]
     top_ref[core, chip] = total
     for k in range(1, chips):
-        push(top_ref.at[core, chip], top_ref.at[core, chip], "t3", k, on_chip(k))
-
-    mark("m_factors")
-    factors_into(fsel_s, lsel_s, found_s, c1, c3)
+        push(top_ref.at[core, chip], top_ref.at[core, chip], "t3", on_chip(k))
+
+    mark("m_bz")
+    arrive(gp_ref.at[0, :planes - 1, :, others], "bz")
     mark("m_gx")
+
+    def chosen_sum(c, z):
+        size = chips * samples
+        at = pl.multiple_of((c * planes + z) * size, size)
+        return dot_parts(
+            gp_ref[pl.ds(c, 1), pl.ds(z, 1)].reshape(size, WIDTH), sample_s[pl.ds(at, size), :], DOWN, 2, 0)
+
+    total = None
     for k in range(planes):
-        grads.relay_x(k)
+        z = back(plane, k, planes)
+        arrive(gp_ref.at[0, 0, :chips - 1, most], "gx", k)
+        push(gp_ref.at[core, z], gp_ref.at[core, z], "gc", on_core(1), planes + k)
+        total = add(total, chosen_sum(core, z))
+    gsel_s[...] = total
 
     mark("m_s2")
 
     def to_owner(p):
         seg = plan.segs[p]
         return remote(seg3.at[:seg.rows], seg_ref.at[core, chip, :seg.rows], "s3",
-                      core * chips + chip, (seg.owner, plane))
+                      (seg.owner, plane))
 
     for p in range(planes):
         @pl.when(plane == p)
         def _(p=p):
             seg = plan.segs[p]
+            arrive(segz.at[1:, :seg.rows], "s2")
             total = seg2[seg.offset:seg.offset + seg.rows]
             for k in range(1, planes):
-                arrive(segz.at[k, :seg.rows], "s2", k)
                 total = total + segz[k, :seg.rows]
             seg3[:seg.rows] = total
 
@@ -598,22 +622,21 @@
                 to_owner(p).start()
 
     mark("m_gfin")
+    total = gsel_s[...]
     for k in range(planes):
-        grads.finish(k)
+        arrive(gp_ref.at[0, 0], "gc", planes + k)
+        total = total + chosen_sum(1 - core, back(plane, k, planes))
+    gsel_s[...] = total
     saves = [pltpu.make_async_copy(digits_ref, digits_out, save_sems.at[0]),
              pltpu.make_async_copy(gp_ref, gp_out, save_sems.at[1])]
     for save in saves:
         save.start()
+    mark("m_t3")
+    arrive(top_ref.at[0, 1:], "t3")
+    push(top_ref.at[core], top_ref.at[core], "t4", on_core(1))
+
     mark("m_mid")
-    mid_ref[...] = middle_sum(
-        plan, gp_ref[...].reshape(groups * samples, WIDTH), samples,
-        found_s, fsel_s, lsel_s, gsel_s, glsel_s)
-
-    mark("m_t3")
-    for k in range(1, chips):
-        arrive(top_ref.at[core, back(chip, k, chips)], "t3", k)
-    for c in range(1, cores):
-        push(top_ref.at[core], top_ref.at[core], "t4", c, on_core(c))
+    mid_ref[...] = middle_sum(plan, spread_s, lsel_s, gsel_s, glsel_s)
 
     mark("m_s3")
     for p in range(planes):
@@ -623,26 +646,31 @@
         def _(p=p, seg=seg):
             own_core, own_chip = seg.owner % cores, seg.owner // cores
             seg_ref[own_core, own_chip, :seg.rows] = seg3[:seg.rows]
-            for c in range(cores):
-                for q in range(chips):
-                    if (c, q) != (own_core, own_chip):
-                        arrive(seg_ref.at[c, q, :seg.rows], "s3", c * chips + q)
+            arrive(segall.at[:(cores * chips - 1) * seg.rows], "s3")
 
     mark("m_t4")
-    for c in range(1, cores):
-        arrive(top_ref.at[back(core, c, cores)], "t4", c)
+    arrive(top_ref.at[1 - core], "t4")
     mark("m_sent")
     for save in saves:
         save.wait()
-    for copy in sent:
-        copy.wait_send()
+    for kind, ref in (("d", digits_ref), ("g", gp_ref)):
+        rows = most if kind == "g" else slice(None)
+        leave(of_z(ref, rows), kind + "z")
+        leave(of_x(ref, rows), kind + "x")
+        leave(ref.at[0], kind + "c")
+    leave(gp_ref.at[0, 0, :chips - 1, others], "bx")
+    leave(gp_ref.at[0, :planes - 1, :, others], "bz")
+    for stage, like in (
+        ("t0", topin), ("t1", topx.at[1:]), ("t2", topz.at[1:]), ("t3", top_ref.at[0, 1:]),
+        ("t4", top_ref.at[0]), ("s0", segin), ("s1", segx.at[1:])):
+        leave(like, stage)
     for p in range(planes):
         @pl.when(plane == p)
         def _(p=p):
-            for k in range(1, planes):
-                out_of(p, k).wait_send()
-
-            @pl.when(gx != plan.segs[p].owner)
+            seg = plan.segs[p]
+            leave(seg2.at[:plan.srows - seg.rows], "s2")
+
+            @pl.when(gx != seg.owner)
             def _():
                 to_owner(p).wait_send()
     mark(None)
@@ -661,9 +689,9 @@
     grads = (cores, planes, chips, samples, WIDTH)
     sums = [
         digits, grads,
-        (cores, chips, *top), (cores, chips, *top), (chips, *top), (chips, *top), (planes, *top),
-        (cores, chips, *seg), (cores, chips, *seg), (chips, *seg), (chips, *seg), seg,
-        (planes, plan.smost, LANES), (plan.smost, LANES)]
+        (cores, chips, *top), (chips, *top), (chips, *top), (chips, *top), (planes, *top),
+        (cores, chips, *seg), (chips, *seg), (chips, *seg), (chips, *seg), seg,
+        (planes, plan.smost, LANES), (plan.smost, LANES), (cores * chips * plan.smost, LANES)]
     inputs = [pltpu.with_memory_space_constraint(x, pltpu.HBM) for x in inputs]
     return pl.pallas_call(
         functools.partial(step_kernel, plan),
@@ -680,9 +708,11 @@
         scratch_shapes=[pltpu.VMEM(x.shape, x.dtype) for x in inputs]
         + [pltpu.VMEM((rows, looks), F32) for rows in scratch]
         + [pltpu.VMEM(dims, F32) for dims in sums]
-        + select_scratch(groups, looks, chunk)
-        + [pltpu.SemaphoreType.DMA((len(inputs) + 3,)), pltpu.SemaphoreType.DMA((2,))]
-        + [pltpu.SemaphoreType.DMA((size,)) for size in stage_sizes(plan) for _ in range(2)],
+        + select_scratch(plan, looks, samples, chunk)
+        + [pltpu.VMEM((groups, looks), jnp.int32), pltpu.VMEM((groups * LOCAL, 8), F32)]
+        + [pltpu.SemaphoreType.DMA((len(inputs) + 1,)), pltpu.SemaphoreType.DMA((2,))]
+        + [pltpu.SemaphoreType.DMA((len(STAGES),)) for _ in range(2)]
+        + [pltpu.SemaphoreType.DMA((2 * planes,))],
         compiler_params=pltpu.CompilerParams(
             collective_id=0, has_side_effects=True, vmem_limit_bytes=40 << 20),
         name="step",
@@ -690,8 +720,8 @@
 
 
 def finish_kernel(
-    plan, c1_in, c3_in, digits_in, gp_in, top, seg_in, mid, count_in, core_out, top_out,
-    c1, c3, blocks_s, gp_s, rank_s, vals_s, found_s, fsel_s, lsel_s, gsel_s, glsel_s,
+    plan, c1_in, c3_in, digits_in, gp_in, top, seg_in, mid, rest_in, core_out, top_out,
+    c1, c3, blocks_s, gp_s, rank_s, vals_s, found_s, spread_s, lsel_s, sample_s, gsel_s, glsel_s,
     big_s, core_s, top_s, more_sems, out_sems,
 ):
     cores, chips, planes, window = plan.cores, plan.chips, plan.planes, plan.window
@@ -710,9 +740,8 @@
 
     base, rows = plan.n1 // LANES, window * R
     big_s[base:base + rows, :] = mid[...]
-    count = jnp.max(count_in[...]).astype(jnp.int32)
-
-    @pl.when(count > chunk)
+
+    @pl.when(jnp.max(rest_in[...]) > 0.0)
     def _():
         pairs = zip((c1_in, c3_in, digits_in, gp_in), (c1, c3, blocks_s, gp_s))
         loads = [pltpu.make_async_copy(a, b, more_sems.at[k]) for k, (a, b) in enumerate(pairs)]
@@ -721,17 +750,21 @@
         for load in loads:
             load.wait()
         groups, samples = rank_s.shape[0], gp_s.shape[3]
-        rank_lookups(plan, blocks_s[...].reshape(groups, *blocks_s.shape[3:]), rank_s, vals_s)
+        count, _ = rank_lookups(
+            plan, blocks_s[...].reshape(groups, *blocks_s.shape[3:]), rank_s, vals_s)
+        count = jnp.max(count).astype(jnp.int32)
+        big_s[base:base + rows, :] = jnp.zeros((rows, LANES), F32)
 
         def body(step, carry):
             pick_into(found_s, step, rank_s, vals_s)
-            factors_into(fsel_s, lsel_s, found_s, c1, c3)
+            factors_into(plan, samples, spread_s, lsel_s, sample_s, found_s, c1, c3)
+            gsel_s[...] = dot_parts(
+                gp_s[...].reshape(groups * samples, WIDTH), sample_s[...], DOWN, 2, 0)
             big_s[base:base + rows, :] = big_s[base:base + rows, :] + middle_sum(
-                plan, gp_s[...].reshape(groups * samples, WIDTH), samples,
-                found_s, fsel_s, lsel_s, gsel_s, glsel_s)
+                plan, spread_s, lsel_s, gsel_s, glsel_s)
             return carry
 
-        lax.fori_loop(1, (count + chunk - 1) // chunk, body, 0)
+        lax.fori_loop(0, (count + chunk - 1) // chunk, body, 0)
 
     halves = seg_in.shape[0]
     for p in range(planes):
@@ -760,8 +793,7 @@
     save_core.wait()
 
 
-def finish_part(plan, chunk, looks, c1, c3, digits, gp, top, seg, mid, count):
-    groups = plan.cores * plan.chips * plan.planes
+def finish_part(plan, chunk, looks, c1, c3, digits, gp, top, seg, mid, rest):
     vmem = pl.BlockSpec(memory_space=pltpu.VMEM)
     hbm = pl.BlockSpec(memory_space=pltpu.HBM)
     out_rows = up(-(-plan.share // LANES), 8)
@@ -775,21 +807,21 @@
         in_specs=[hbm] * 4 + [vmem] * 4,
         out_specs=(hbm, hbm),
         scratch_shapes=[pltpu.VMEM(x.shape, x.dtype) for x in (c1, c3, digits, gp)]
-        + select_scratch(groups, looks, chunk)
+        + select_scratch(plan, looks, gp.shape[3], chunk)
         + [pltpu.VMEM((big, LANES), F32), pltpu.VMEM(core_shape, F32),
            pltpu.VMEM(top_shape, F32), pltpu.SemaphoreType.DMA((4,)), pltpu.SemaphoreType.DMA((2,))],
         compiler_params=pltpu.CompilerParams(vmem_limit_bytes=40 << 20),
         name="finish",
-    )(*far, top, seg, mid, count)
+    )(*far, top, seg, mid, rest)
 
 
 def per_device(plan, c1, c2, c3, dense, w, bias, wout, labels, bag, d1, d2, d3):
     looks = d1.shape[1]
     expected = plan.nx * plan.ny * looks * plan.window // plan.n2_rows
     chunk = up(expected * 9 // 8, LANES)
-    digits, gp, top, seg, mid, count = step_part(
+    digits, gp, top, seg, mid, rest = step_part(
         plan, chunk, c1, c2, c3, dense, w, bias[None], wout[None], labels[None], bag, d1, d2, d3)
-    core, top = finish_part(plan, chunk, looks, c1, c3, digits, gp, top, seg, mid, count)
+    core, top = finish_part(plan, chunk, looks, c1, c3, digits, gp, top, seg, mid, rest)
     return core.reshape(-1)[:plan.share], top
 
 

time: 33.1 us -> 26.9 us (0.81)
  Pallas kernels: 32.3 us -> 26.1 us
    pallas_call x1, Pallas kernels: 31.3 us -> 25.1 us  [step_part(): pl.pallas_call(functools.partial(step_kernel, plan), in_specs=[hbm] * len...]
where the time goes in v2:
time: 26.9 us; the launch traced here: 26.7 us
  Pallas kernels  26.1 us (97%)
  between operations  0.64 us (2%)
    pallas_call x1, Pallas kernels, step_part(): pl.pallas_call(functools.partial(step_kernel, plan), in_specs=[hbm] * len...  25.1 us
    pallas_call x1, Pallas kernels, finish_part(): pl.pallas_call(functools.partial(finish_kernel, plan), out_shape=(pltpu.H...  0.98 us

profile of v2, /device:TPU:0, one launch (start us, length us, event | category | flops | bytes accessed | tf_op | source)
XLA Modules:
  0.0 26.7 jit_solution(13133603750866245122)
XLA Ops:
  0.6 25.1 %step.1 = (f32[2,4,4,8,128]{4,3,2,1,0:T(8,128)}, f32[2,4,4,64,128]{4,3,2,1,0:T(8,128)}, f32[2,4,72,128]{3,2,1,0:T(8,128)S(1)}, f32[2,4,32,128]{3,2,1,0:T(8,128)S...) custom-call(bf16[200,128]{1,0:T(8,128)(2,1)} %c1_in.1, bf16[200,4096]{1,0:T(8,128)(2,1)} %refs_1_.1, ...), custom_call_target="tpu_custom_call" | custom-call | tf_op jit(solution)/shard_map/step/pallas_call | solution.py:696
  25.8 1.0 %finish.1 = (f32[224,128]{1,0:T(8,128)}, f32[258,256]{1,0:T(8,128)}) custom-call(bf16[200,128]{1,0:T(8,128)(2,1)} %c1_in.1, bf16[250,256]{1,0:T(8,128)(2,1)} %c3_in.1, f32[2,4,4,8,128]{4,3,2,1,0:T(8,128)} %get-tuple-element.10.digits_in, f32[2,4,4,64,128]{4,3,2,1,0:T(8,128)} %get-tuple-element.11.gp_in, f32[2,4,72,128]{3,2,1,0:T(8,128)S(1)} %get-tuple-element.12.top, ...), custom_call_target="tpu_custom_call" | custom-call | tf_op jit(solution)/shard_map/finish/pallas_call | solution.py:804

commit v3 on v2

--- a/solution.py
+++ b/solution.py
@@ -101,12 +101,12 @@
         segs[d % planes] = seg
     if any(seg is None for seg in segs):
         return None
-    for seg in segs:
+    for seg in sorted(segs, key=lambda seg: not seg.first):
         seg.offset = offset
         offset += seg.rows
     return types.SimpleNamespace(
         nx=nx, ny=ny, cores=cores, chips=chips, planes=planes, share=share, window=window,
-        row=row, n1=n1, segs=segs, srows=offset, smost=max(seg.rows for seg in segs),
+        row=row, n1=n1, segs=segs, srows=offset, frows=sum(seg.rows for seg in segs if seg.first), smost=max(seg.rows for seg in segs),
         trows=shape_top[0] // chips + 8, n2_rows=shape_two[0], n3_rows=shape_three[0])
 
 
@@ -124,10 +124,10 @@
     return [(lo, min(step, count - lo)) for lo in range(0, count, step)]
 
 
-def lane_loop(count, lanes, body):
+def lane_loop(count, lanes, body, start=0):
     blocks = lanes // LANES
 
-    @pl.loop(0, count * blocks)
+    @pl.loop(start * blocks, count * blocks)
     def _(step):
         body(step // blocks, pl.ds(pl.multiple_of((step % blocks) * LANES, LANES), LANES))
 
@@ -193,7 +193,7 @@
             gl_s[pl.ds(pl.multiple_of((b * batch + k) * D3, D3), D3), :] = totals[k]
 
 
-def grad_first_into(gf_s, gleft_s, mid_s, batch=8):
+def grad_first_into(gf_s, gleft_s, mid_s, part, parts, batch=8):
     def body(b, lanes):
         totals = [[None] * D1 for _ in range(batch)]
         size = batch * SIDE
@@ -210,7 +210,8 @@
             gf_s[pl.ds(pl.multiple_of(i * R + b * batch, 8), batch), lanes] = (
                 jnp.concatenate(rows, axis=0))
 
-    lane_loop(R // batch, gf_s.shape[1], body)
+    count = R // batch
+    lane_loop((part + 1) * count // parts, gf_s.shape[1], body, part * count // parts)
 
 
 def first_row(plan):
@@ -317,7 +318,7 @@
     ]
 
 
-STAGES = ("dz", "dx", "dc", "gz", "gx", "gc", "bx", "bz", "t0", "t1", "t2", "t3", "t4", "s0", "s1", "s2", "s3")
+STAGES = ("dz", "dx", "dc", "gz", "gx", "gc", "t0", "t1", "t2", "t3", "t4", "l0", "l1", "f0", "f1", "s2", "s3")
 
 
 def step_kernel(plan, *refs):
@@ -414,6 +415,7 @@
     def of_x(ref, rows=slice(None)):
         return ref.at[0, :, :chips - 1, rows]
 
+    seg_s[...] = jnp.zeros_like(seg_s)
     mark("m_gather")
     for n in early:
         loads[n].wait()
@@ -435,10 +437,6 @@
         for lo, size in spans(wide, 512):
             lo += k * wide
             mid_s[lo:lo + size, :] = dot(c2[:, lo:lo + size], hot2, DOWN)
-    mark("m_barrier")
-    pl.semaphore_wait(barrier, len(peers))
-    own_z(digits_ref, "d")
-    push_x(digits_ref, "d", 0)
     mark("m_left")
     left_into(left_s, first_s, mid_s)
     for n in late:
@@ -478,18 +476,62 @@
             half = weight[lo // WIDTH]
             top_s[h, q, :deep, :] = half[lo % WIDTH:lo % WIDTH + deep, lanes]
             top_s[h, q, deep:, :] = vectors[:, lanes] if q == 0 else jnp.zeros((8, LANES), F32)
+    mark("m_barrier")
+    pl.semaphore_wait(barrier, len(peers))
+    mark("m_send")
     push(top_s.at[1 - core], topin, "t0", on_core(1))
+    push_x(digits_ref, "d", 0)
     gp = dot(low, w[WIDTH:, :], ACROSS)
     gp_ref[core, plane, chip] = gp
-    split = samples - samples // 4
-    most, others = slice(0, split), slice(split, samples)
-    push_x(gp_ref, "b", 0, None, others)
+    most = slice(None)
     own_z(gp_ref, "g", most)
 
     mark("m_gleft")
     g_s[...] = dot_parts(gp, bags, DOWN, 2, 0)
     mark("m_gl")
     grad_last_into(gl_s, left_s, g_s)
+
+    def seg_rows(first):
+        return slice(0, plan.frows) if first else slice(plan.frows, plan.srows)
+
+    def seg_start(first, value):
+        for seg in plan.segs:
+            if seg.first == first:
+                for c, q, lo, hi, h in pieces_of(seg, cores, chips, cores):
+                    seg_s[c, q, seg.offset:seg.offset + hi - lo, :] = (
+                        value[lo:hi, h * LANES:(h + 1) * LANES])
+        rows = seg_rows(first)
+        push(seg_s.at[1 - core, :, rows], segin.at[:, rows], "f0" if first else "l0", on_core(1))
+
+    def seg_chips(first):
+        rows = seg_rows(first)
+        arrive(segin.at[:, rows], "f0" if first else "l0")
+        seg1[:, rows] = seg_s[core, :, rows] + segin[:, rows]
+        for k in range(1, chips):
+            push(seg1.at[(chip + k) % chips, rows], segx.at[k, rows],
+                 "f1" if first else "l1", on_chip(k))
+
+    def out_of(p, k):
+        seg = plan.segs[(p + k) % planes]
+        return remote(seg2.at[seg.offset:seg.offset + seg.rows],
+                      segz.at[k, :seg.rows], "s2", on_plane(k))
+
+    def seg_planes(first):
+        rows = seg_rows(first)
+        arrive(segx.at[1:, rows], "f1" if first else "l1")
+        total = seg1[chip, rows]
+        for k in range(1, chips):
+            total = total + segx[k, rows]
+        seg2[rows] = total
+        for p in range(planes):
+            @pl.when(plane == p)
+            def _(p=p):
+                for k in range(1, planes):
+                    if plan.segs[(p + k) % planes].first == first:
+                        out_of(p, k).start()
+
+    mark("m_ldot")
+    seg_start(False, dot_parts(hot3, gl_s[...], ACROSS, 2, 1))
     mark("m_gleft2")
     grad_left_into(gleft_s, g_s, lastd_s)
     mark("m_t0")
@@ -497,34 +539,22 @@
     top1[...] = top_s[core] + topin[...]
     for k in range(1, chips):
         push(top1.at[(chip + k) % chips], topx.at[k], "t1", on_chip(k))
-    mark("m_dz")
-    arrive(of_z(digits_ref), "dz")
+    push_x(gp_ref, "g", 0, 0, most)
+
+    mark("m_gf")
+    grad_first_into(gf_s, gleft_s, mid_s, 0, 2)
+    mark("m_l0")
+    seg_chips(False)
+    mark("m_dx")
+    arrive(digits_ref.at[0, 0, :chips - 1], "dx")
     for k in range(1, planes):
-        push_x(digits_ref, "d", k)
-    push_x(gp_ref, "g", 0, 0, most)
-
-    mark("m_gf")
-    grad_first_into(gf_s, gleft_s, mid_s)
-    mark("m_segdot")
-    sums = {True: dot_parts(hot1, gf_s[...], ACROSS, 2, 1),
-            False: dot_parts(hot3, gl_s[...], ACROSS, 2, 1)}
-    seg_s[...] = jnp.zeros_like(seg_s)
-    for seg in plan.segs:
-        for c, q, lo, hi, h in pieces_of(seg, cores, chips, cores):
-            seg_s[c, q, seg.offset:seg.offset + hi - lo, :] = (
-                sums[seg.first][lo:hi, h * LANES:(h + 1) * LANES])
-    push(seg_s.at[1 - core], segin, "s0", on_core(1))
-
-    mark("m_bx")
-    arrive(gp_ref.at[0, 0, :chips - 1, others], "bx")
-    slot = gp_ref.at[core, plane, :, others]
-    for k in range(1, planes):
-        push(slot, slot, "bz", on_plane(k))
-    mark("m_s0")
-    arrive(segin, "s0")
-    seg1[...] = seg_s[core] + segin[...]
-    for k in range(1, chips):
-        push(seg1.at[(chip + k) % chips], segx.at[k], "s1", on_chip(k))
+        push(digits_ref.at[core, plane], digits_ref.at[core, plane], "dz", on_plane(k))
+    mark("m_gf2")
+    grad_first_into(gf_s, gleft_s, mid_s, 1, 2)
+    mark("m_fdot")
+    seg_start(True, dot_parts(hot1, gf_s[...], ACROSS, 2, 1))
+    mark("m_f0")
+    seg_chips(True)
 
     mark("m_gz")
     arrive(of_z(gp_ref, most), "gz")
@@ -539,8 +569,8 @@
     for k in range(1, planes):
         push(topz.at[plane], topz.at[plane], "t2", on_plane(k))
 
-    mark("m_dx")
-    arrive(of_x(digits_ref), "dx")
+    mark("m_dz")
+    arrive(digits_ref.at[0, :planes - 1], "dz")
     push(digits_ref.at[core], digits_ref.at[core], "dc", on_core(1))
     mark("m_df")
     arrive(digits_ref.at[1 - core], "dc")
@@ -553,24 +583,10 @@
     mark("m_pick")
     pick_few_into(found_s, local_s, vals_s, few_s)
 
-    mark("m_s1")
-    arrive(segx.at[1:], "s1")
-    total = seg1[chip]
-    for k in range(1, chips):
-        total = total + segx[k]
-    seg2[...] = total
-
-    def out_of(p, k):
-        seg = plan.segs[(p + k) % planes]
-        return remote(seg2.at[seg.offset:seg.offset + seg.rows],
-                      segz.at[k, :seg.rows], "s2", on_plane(k))
-
-    for p in range(planes):
-        @pl.when(plane == p)
-        def _(p=p):
-            for k in range(1, planes):
-                out_of(p, k).start()
-
+    mark("m_l1")
+    seg_planes(False)
+    mark("m_f1")
+    seg_planes(True)
     mark("m_factors")
     factors_into(plan, samples, spread_s, lsel_s, sample_s, found_s, c1, c3)
     mark("m_t2")
@@ -582,23 +598,19 @@
     for k in range(1, chips):
         push(top_ref.at[core, chip], top_ref.at[core, chip], "t3", on_chip(k))
 
-    mark("m_bz")
-    arrive(gp_ref.at[0, :planes - 1, :, others], "bz")
     mark("m_gx")
 
-    def chosen_sum(c, z):
-        size = chips * samples
-        at = pl.multiple_of((c * planes + z) * size, size)
+    def chosen_sum(c):
+        size = planes * chips * samples
         return dot_parts(
-            gp_ref[pl.ds(c, 1), pl.ds(z, 1)].reshape(size, WIDTH), sample_s[pl.ds(at, size), :], DOWN, 2, 0)
-
-    total = None
+            gp_ref[c].reshape(size, WIDTH), sample_s[pl.ds(pl.multiple_of(c * size, size), size), :],
+            DOWN, 2, 0)
+
     for k in range(planes):
-        z = back(plane, k, planes)
+        slot = gp_ref.at[core, back(plane, k, planes)]
         arrive(gp_ref.at[0, 0, :chips - 1, most], "gx", k)
-        push(gp_ref.at[core, z], gp_ref.at[core, z], "gc", on_core(1), planes + k)
-        total = add(total, chosen_sum(core, z))
-    gsel_s[...] = total
+        push(slot, slot, "gc", on_core(1), planes + k)
+    gsel_s[...] = chosen_sum(core)
 
     mark("m_s2")
 
@@ -621,20 +633,18 @@
             def _():
                 to_owner(p).start()
 
+    mark("m_t3")
+    arrive(top_ref.at[0, 1:], "t3")
+    push(top_ref.at[core], top_ref.at[core], "t4", on_core(1))
+
     mark("m_gfin")
-    total = gsel_s[...]
     for k in range(planes):
         arrive(gp_ref.at[0, 0], "gc", planes + k)
-        total = total + chosen_sum(1 - core, back(plane, k, planes))
-    gsel_s[...] = total
+    gsel_s[...] = gsel_s[...] + chosen_sum(1 - core)
     saves = [pltpu.make_async_copy(digits_ref, digits_out, save_sems.at[0]),
              pltpu.make_async_copy(gp_ref, gp_out, save_sems.at[1])]
     for save in saves:
         save.start()
-    mark("m_t3")
-    arrive(top_ref.at[0, 1:], "t3")
-    push(top_ref.at[core], top_ref.at[core], "t4", on_core(1))
-
     mark("m_mid")
     mid_ref[...] = middle_sum(plan, spread_s, lsel_s, gsel_s, glsel_s)
 
@@ -653,16 +663,17 @@
     mark("m_sent")
     for save in saves:
         save.wait()
-    for kind, ref in (("d", digits_ref), ("g", gp_ref)):
-        rows = most if kind == "g" else slice(None)
-        leave(of_z(ref, rows), kind + "z")
-        leave(of_x(ref, rows), kind + "x")
-        leave(ref.at[0], kind + "c")
-    leave(gp_ref.at[0, 0, :chips - 1, others], "bx")
-    leave(gp_ref.at[0, :planes - 1, :, others], "bz")
+    leave(digits_ref.at[0, 0, :chips - 1], "dx")
+    leave(digits_ref.at[0, :planes - 1], "dz")
+    leave(of_z(gp_ref, most), "gz")
+    leave(of_x(gp_ref, most), "gx")
+    for ref, stage in ((digits_ref, "dc"), (gp_ref, "gc")):
+        leave(ref.at[0], stage)
     for stage, like in (
         ("t0", topin), ("t1", topx.at[1:]), ("t2", topz.at[1:]), ("t3", top_ref.at[0, 1:]),
-        ("t4", top_ref.at[0]), ("s0", segin), ("s1", segx.at[1:])):
+        ("t4", top_ref.at[0]), ("l0", segin.at[:, seg_rows(False)]),
+        ("l1", segx.at[1:, seg_rows(False)]), ("f0", segin.at[:, seg_rows(True)]),
+        ("f1", segx.at[1:, seg_rows(True)])):
         leave(like, stage)
     for p in range(planes):
         @pl.when(plane == p)

time: 26.9 us -> 26.7 us (level)
  no operation moved by 1% of the time
where the time goes in v3:
time: 26.7 us; the launch traced here: 26.6 us
  Pallas kernels  25.9 us (97%)
  between operations  0.64 us (2%)
    pallas_call x1, Pallas kernels, step_part(): pl.pallas_call(functools.partial(step_kernel, plan), in_specs=[hbm] * len...  24.9 us
    pallas_call x1, Pallas kernels, finish_part(): pl.pallas_call(functools.partial(finish_kernel, plan), out_shape=(pltpu.H...  0.98 us

profile of v3, /device:TPU:0, one launch (start us, length us, event | category | flops | bytes accessed | tf_op | source)
XLA Modules:
  0.0 26.6 jit_solution(9921845466088351175)
XLA Ops:
  0.6 24.9 %step.1 = (f32[2,4,4,8,128]{4,3,2,1,0:T(8,128)}, f32[2,4,4,64,128]{4,3,2,1,0:T(8,128)}, f32[2,4,72,128]{3,2,1,0:T(8,128)S(1)}, f32[2,4,32,128]{3,2,1,0:T(8,128)S...) custom-call(bf16[200,128]{1,0:T(8,128)(2,1)} %c1_in.1, bf16[200,4096]{1,0:T(8,128)(2,1)} %refs_1_.1, ...), custom_call_target="tpu_custom_call" | custom-call | tf_op jit(solution)/shard_map/step/pallas_call | solution.py:707
  25.6 1.0 %finish.1 = (f32[224,128]{1,0:T(8,128)}, f32[258,256]{1,0:T(8,128)}) custom-call(bf16[200,128]{1,0:T(8,128)(2,1)} %c1_in.1, bf16[250,256]{1,0:T(8,128)(2,1)} %c3_in.1, f32[2,4,4,8,128]{4,3,2,1,0:T(8,128)} %get-tuple-element.10.digits_in, f32[2,4,4,64,128]{4,3,2,1,0:T(8,128)} %get-tuple-element.11.gp_in, f32[2,4,72,128]{3,2,1,0:T(8,128)S(1)} %get-tuple-element.12.top, ...), custom_call_target="tpu_custom_call" | custom-call | tf_op jit(solution)/shard_map/finish/pallas_call | solution.py:815

commit v4 on v3

--- a/solution.py
+++ b/solution.py
@@ -539,7 +539,6 @@
     top1[...] = top_s[core] + topin[...]
     for k in range(1, chips):
         push(top1.at[(chip + k) % chips], topx.at[k], "t1", on_chip(k))
-    push_x(gp_ref, "g", 0, 0, most)
 
     mark("m_gf")
     grad_first_into(gf_s, gleft_s, mid_s, 0, 2)
@@ -549,6 +548,7 @@
     arrive(digits_ref.at[0, 0, :chips - 1], "dx")
     for k in range(1, planes):
         push(digits_ref.at[core, plane], digits_ref.at[core, plane], "dz", on_plane(k))
+    push_x(gp_ref, "g", 0, 0, most)
     mark("m_gf2")
     grad_first_into(gf_s, gleft_s, mid_s, 1, 2)
     mark("m_fdot")
@@ -609,7 +609,7 @@
     for k in range(planes):
         slot = gp_ref.at[core, back(plane, k, planes)]
         arrive(gp_ref.at[0, 0, :chips - 1, most], "gx", k)
-        push(slot, slot, "gc", on_core(1), planes + k)
+        push(slot, slot, "gc", on_core(1))
     gsel_s[...] = chosen_sum(core)
 
     mark("m_s2")
@@ -638,8 +638,7 @@
     push(top_ref.at[core], top_ref.at[core], "t4", on_core(1))
 
     mark("m_gfin")
-    for k in range(planes):
-        arrive(gp_ref.at[0, 0], "gc", planes + k)
+    arrive(gp_ref.at[0], "gc")
     gsel_s[...] = gsel_s[...] + chosen_sum(1 - core)
     saves = [pltpu.make_async_copy(digits_ref, digits_out, save_sems.at[0]),
              pltpu.make_async_copy(gp_ref, gp_out, save_sems.at[1])]
@@ -723,7 +722,7 @@
         + [pltpu.VMEM((groups, looks), jnp.int32), pltpu.VMEM((groups * LOCAL, 8), F32)]
         + [pltpu.SemaphoreType.DMA((len(inputs) + 1,)), pltpu.SemaphoreType.DMA((2,))]
         + [pltpu.SemaphoreType.DMA((len(STAGES),)) for _ in range(2)]
-        + [pltpu.SemaphoreType.DMA((2 * planes,))],
+        + [pltpu.SemaphoreType.DMA((planes,))],
         compiler_params=pltpu.CompilerParams(
             collective_id=0, has_side_effects=True, vmem_limit_bytes=40 << 20),
         name="step",

time: 26.7 us -> 26.5 us (level)
  no operation moved by 1% of the time
where the time goes in v4:
time: 26.5 us; the launch traced here: 26.3 us
  Pallas kernels  25.7 us (97%)
  between operations  0.64 us (2%)
    pallas_call x1, Pallas kernels, step_part(): pl.pallas_call(functools.partial(step_kernel, plan), in_specs=[hbm] * len...  24.7 us
    pallas_call x1, Pallas kernels, finish_part(): pl.pallas_call(functools.partial(finish_kernel, plan), out_shape=(pltpu.H...  0.98 us

profile of v4, /device:TPU:0, one launch (start us, length us, event | category | flops | bytes accessed | tf_op | source)
XLA Modules:
  0.0 26.3 jit_solution(13143418144675724910)
XLA Ops:
  0.6 24.7 %step.1 = (f32[2,4,4,8,128]{4,3,2,1,0:T(8,128)}, f32[2,4,4,64,128]{4,3,2,1,0:T(8,128)}, f32[2,4,72,128]{3,2,1,0:T(8,128)S(1)}, f32[2,4,32,128]{3,2,1,0:T(8,128)S...) custom-call(bf16[200,128]{1,0:T(8,128)(2,1)} %c1_in.1, bf16[200,4096]{1,0:T(8,128)(2,1)} %refs_1_.1, ...), custom_call_target="tpu_custom_call" | custom-call | tf_op jit(solution)/shard_map/step/pallas_call | solution.py:706
  25.3 1.0 %finish.1 = (f32[224,128]{1,0:T(8,128)}, f32[258,256]{1,0:T(8,128)}) custom-call(bf16[200,128]{1,0:T(8,128)(2,1)} %c1_in.1, bf16[250,256]{1,0:T(8,128)(2,1)} %c3_in.1, f32[2,4,4,8,128]{4,3,2,1,0:T(8,128)} %get-tuple-element.10.digits_in, f32[2,4,4,64,128]{4,3,2,1,0:T(8,128)} %get-tuple-element.11.gp_in, f32[2,4,72,128]{3,2,1,0:T(8,128)S(1)} %get-tuple-element.12.top, ...), custom_call_target="tpu_custom_call" | custom-call | tf_op jit(solution)/shard_map/finish/pallas_call | solution.py:814
